TPU v7x, 32 devices: a whole 2x2x4 slice. The times are simulated.
32 devices in a mesh: dp: 8 (over z, y), feat: 4 (over x, core).
Axes of the slice: x: 2, y: 2, z: 4, core: 2. Of those that a mesh axis runs over, the one named last changes fastest.
Arguments:
- observations: bfloat16 [1024, 128, 128], P('dp', 'feat'), may hold values from -1.5 to 1.5
- labels: int32 [1024, 128], P('dp'), may hold values 0 or 1
- tile_live: int32 [1024], P('dp'), may hold values from 1 to 128
- tile_group: int32 [1024], P('dp'), may hold values from 0 to 127, as said below
- position: float32 [128, 2048], P('dp', 'feat'), may hold values from -2.4 to 2.4
- momentum: float32 [128, 2048], P('dp', 'feat'), may hold values from -6 to 6
- gradient: float32 [128, 2048], P('dp', 'feat'), may hold values from -18 to 18
- prior_mean: float32 [2048], P('feat'), may hold values from -1.8 to 1.8
- prior_prec: float32 [128], P('feat'), may hold values from 0.25 to 4
- inv_mass: float32 [128], P('feat'), may hold values from 0.5 to 2
Outputs:
- new_position: float32 [128, 2048], P('dp', 'feat')
- new_momentum: float32 [128, 2048], P('dp', 'feat')
- new_gradient: float32 [128, 2048], P('dp', 'feat')
- energy: float32 [128, 16], P('dp')
Inputs may be any that keep to these rules, and one draw needn't show every extreme that they name: `tile_group`: group g belongs to owner g // 16. Among the 128 tiles of one device at most 32 have groups of any one owner, and one owner has exactly 32 tiles from every device. `tile_live`: the live slots of a tile come first.
All inputs are finite; a program needn't handle non-finite values. No bound on the sum of `labels` on one device may be relied on, other than what follows from the above.
Results may differ from a plain program's by a relative error of at most 0.0041.
Values may be sent and summed in bfloat16 or wider, within the bound.
A program may use at most 64 MiB of HBM per device.

v0:
```python
import functools
import jax
import jax.numpy as jnp
from jax import lax
from jax.experimental import pallas as pl
from jax.experimental.pallas import tpu as pltpu
from jax.sharding import PartitionSpec as P

step_size = 0.1
LANES = 128
CHUNKS = 8
MESH = pl.DeviceIdType.MESH
BF16 = jnp.bfloat16
F32 = jnp.float32


def iota(shape, dim):
    return lax.broadcasted_iota(jnp.int32, shape, dim)


def split(x):
    hi = x.astype(BF16)
    return hi, (x - hi.astype(F32)).astype(BF16)


def nt_dot(a, b):
    return lax.dot_general(a, b, (((1,), (1,)), ((), ())), preferred_element_type=F32)


def kernel(
    n, nf, chains, quarter,
    obs_hbm, lab_hbm, live_hbm, grp_hbm, pos_hbm, mom_hbm, grad_hbm, mean_hbm, prec_hbm, mass_hbm,
    newpos_out, newmom_out, newgrad_out, energy_out,
    lab_in, live_ref, grp_ref, pos_ref, mom_ref, grad_ref, mean_ref, pair_ref,
    lab_ref, par_ref, newpos_ref, newmom_ref, newgrad_ref, energy_ref, obs, perm, wsrc, wall, half_ref, lhs, mine, pair_send, pair_recv,
    far_send, far_recv, res_own, res_recv, nll_ref, dmat, gsend0, gsend1, grecv0, grecv1, esend, erecv,
    in_sem, out_sem, w_ssem, w_rsem, p_ssem, p_rsem, f_ssem, f_rsem, r_ssem, r_rsem,
    g_ssem, g_rsem, e_ssem, e_rsem,
):
    me = lax.axis_index("dp")
    feat = lax.axis_index("feat")
    tiles = lab_ref.shape[0]
    own, width = pos_ref.shape
    pack = LANES // quarter
    quads = tiles // pack
    qrows = pack * chains
    half_quads = quads // 2
    chunk_quads = half_quads // CHUNKS
    chunk_tiles = chunk_quads * pack
    crows = chunk_quads * qrows
    groups = n * own
    bit = feat % 2
    near = feat + 1 - 2 * bit
    far = (feat + nf // 2) % nf

    barrier = pltpu.get_barrier_semaphore()

    def greet(i, carry):
        pl.semaphore_signal(barrier, inc=1, device_id={"dp": (me + i) % n}, device_id_type=MESH)
        return carry

    lax.fori_loop(1, n, greet, 0)
    for i in range(1, nf):
        pl.semaphore_signal(barrier, inc=1, device_id={"feat": (feat + i) % nf}, device_id_type=MESH)

    sources = [
        (pos_hbm, pos_ref), (mom_hbm, mom_ref), (grad_hbm, grad_ref), (mean_hbm, mean_ref),
        (prec_hbm, pair_ref.at[0:1]), (mass_hbm, pair_ref.at[1:2]), (grp_hbm, grp_ref),
        (live_hbm, live_ref), (lab_hbm, lab_in), (obs_hbm, obs),
    ]
    fetches = [pltpu.make_async_copy(a, b, in_sem.at[i]) for i, (a, b) in enumerate(sources)]
    for f in fetches:
        f.start()
    spread = (iota((quarter, width), 0) == iota((quarter, width), 1) // chains).astype(F32)
    r, c = iota((width, width), 0), iota((width, width), 1)
    perm[...] = jnp.where(
        (r % chains == c // quarter) & (r // chains == c % quarter), 1.0, 0.0
    ).astype(BF16)
    for f in fetches[:-1]:
        f.wait()
    par_ref[...] = jnp.dot(
        pair_ref[...], spread, precision=lax.Precision.HIGHEST, preferred_element_type=F32
    )
    half = mom_ref[...] - 0.5 * step_size * grad_ref[...]
    half_ref[...] = half
    moved = pos_ref[...] + step_size * par_ref[1:2, :] * half
    newpos_ref[...] = moved
    out_pos = pltpu.make_async_copy(newpos_ref, newpos_out, out_sem.at[0])
    out_pos.start()
    coeff = jnp.dot(moved.astype(BF16), perm[...], preferred_element_type=F32).astype(BF16)
    wsrc[...] = coeff
    own_rows = pl.ds(pl.multiple_of(me * own, own), own)
    wall[own_rows, :] = coeff
    square = iota((tiles, tiles), 0) == iota((tiles, tiles), 1)
    live_col = jnp.sum(jnp.where(square, live_ref[...].astype(F32), 0.0), axis=1, keepdims=True)
    lab_ref[...] = jnp.where(
        iota(lab_ref.shape, 1).astype(F32) < live_col, lab_in[...].astype(F32), -1.0
    )
    nll_ref[...] = jnp.zeros_like(nll_ref)
    pl.semaphore_wait(barrier, n - 1 + nf - 1)

    def w_copy(i):
        to = (me + i) % n
        return pltpu.make_async_remote_copy(
            src_ref=wsrc, dst_ref=wall.at[own_rows], send_sem=w_ssem.at[i],
            recv_sem=w_rsem.at[i], device_id={"dp": to}, device_id_type=MESH,
        )

    def start_w(i, carry):
        w_copy(i).start()
        return carry

    lax.fori_loop(1, n, start_w, 0)
    seg_groups = min(groups, LANES)
    hot = (iota((groups, tiles), 0) == grp_ref[...]).astype(F32).astype(BF16)

    def wait_w(i, carry):
        w_copy(i).wait()
        return carry

    lax.fori_loop(1, n, wait_w, 0)
    picked = lax.dot_general(
        hot, wall[...], (((0,), (0,)), ((), ())), preferred_element_type=F32
    )
    row_t, lane_t = iota((tiles, LANES), 0), iota((tiles, LANES), 1)
    place = row_t % pack
    keep = lane_t // quarter == place
    for m in range(width // LANES):
        x = picked[:, m * LANES:(m + 1) * LANES]
        turned = [x] + [pltpu.roll(x, s * quarter, 1) for s in range(1, pack)]
        for j in range(pack):
            y = turned[0]
            for s in range(1, pack):
                y = jnp.where((place + pack - j) % pack == s, turned[s], y)
            lhs[pl.ds(m * pack + j, tiles, stride=chains), :] = jnp.where(keep, y, 0.0)
    fetches[-1].wait()

    def logits(first_quad, dst, base):
        for i in range(chunk_quads):
            q = first_quad + i
            a = lhs[pl.ds(pl.multiple_of(q * qrows, qrows), qrows), :].astype(BF16)
            dst[pl.ds(pl.multiple_of(base + i * qrows, qrows), qrows), :] = jnp.dot(
                a, obs[q], preferred_element_type=F32
            )

    def rows(k):
        return pl.ds(pl.multiple_of(k * crows, crows), crows)

    def pair_copy(k):
        return pltpu.make_async_remote_copy(
            src_ref=pair_send.at[rows(k)], dst_ref=pair_recv.at[rows(k)],
            send_sem=p_ssem.at[k], recv_sem=p_rsem.at[k],
            device_id={"feat": near}, device_id_type=MESH,
        )

    def far_copy(k):
        return pltpu.make_async_remote_copy(
            src_ref=far_send.at[rows(k)], dst_ref=far_recv.at[rows(k)],
            send_sem=f_ssem.at[k], recv_sem=f_rsem.at[k],
            device_id={"feat": far}, device_id_type=MESH,
        )

    def res_copy(k):
        return pltpu.make_async_remote_copy(
            src_ref=res_own.at[rows(k)], dst_ref=res_recv.at[rows(k)],
            send_sem=r_ssem.at[k], recv_sem=r_rsem.at[k],
            device_id={"feat": near}, device_id_type=MESH,
        )

    def stage_a(k, carry):
        logits((1 - bit) * half_quads + k * chunk_quads, pair_send, k * crows)
        pair_copy(k).start()
        logits(bit * half_quads + k * chunk_quads, mine, k * crows)
        return carry


    def stage_b(k, carry):
        pair_copy(k).wait()
        total = mine[rows(k), :] + pair_recv[rows(k), :]
        mine[rows(k), :] = total
        far_send[rows(k), :] = total.astype(BF16)
        far_copy(k).start()
        return carry

    def stage_ab(k, carry):
        stage_a(k, 0)
        stage_b(k - 1, 0)
        return carry

    stage_a(0, 0)
    lax.fori_loop(1, CHUNKS, stage_ab, 0)
    stage_b(CHUNKS - 1, 0)

    diag = iota((qrows, LANES), 0) // chains == iota((qrows, LANES), 1) // quarter

    def grads(first_quad, src, k):
        for i in range(chunk_quads):
            q = first_quad + i
            a = src[pl.ds(pl.multiple_of(k * crows + i * qrows, qrows), qrows), :]
            g = jnp.where(diag, nt_dot(a, obs[q]), 0.0)
            for j in range(pack):
                dmat[pl.ds(q * pack + j, chains, stride=tiles), :] = g[j * chains:(j + 1) * chains]

    def stage_c(k, carry):
        far_copy(k).wait()
        z = mine[rows(k), :] + far_recv[rows(k), :].astype(F32)
        first = pl.multiple_of((bit * half_quads + k * chunk_quads) * pack, chunk_tiles)
        lab = lab_ref[pl.ds(first, chunk_tiles), :]
        lab = jnp.broadcast_to(lab[:, None, :], (chunk_tiles, chains, LANES)).reshape(crows, LANES)
        live = lab >= 0.0
        e = jnp.exp(-jnp.abs(z))
        inv = 1.0 / (1.0 + e)
        sig = jnp.where(z >= 0.0, inv, e * inv)
        res_own[rows(k), :] = jnp.where(live, sig - lab, 0.0).astype(BF16)
        res_copy(k).start()
        v = jnp.where(live, jnp.maximum(z, 0.0) + jnp.log1p(e) - lab * z, 0.0)
        s = jnp.sum(v, axis=1, keepdims=True) * (2.0 / nf)
        at = iota((crows, LANES), 0) % chains == iota((crows, LANES), 1)
        s = jnp.where(at, s, 0.0).reshape(chunk_tiles, chains, LANES)
        nll_ref[pl.ds(first, chunk_tiles), :] = jnp.sum(s, axis=1)
        grads(bit * half_quads + k * chunk_quads, res_own, k)
        return carry

    lax.fori_loop(0, CHUNKS, stage_c, 0)

    def stage_d(k, carry):
        res_copy(k).wait()
        grads((1 - bit) * half_quads + k * chunk_quads, res_recv, k)
        return carry

    lax.fori_loop(0, CHUNKS, stage_d, 0)

    lane_g = iota((seg_groups, LANES), 1) // quarter
    count = width // LANES
    cut = count // 2
    sums = ((gsend0, grecv0, range(cut), True), (gsend1, grecv1, range(cut, count), False))

    def stacked(d):
        return jnp.concatenate(split(d), axis=0)

    def segment(gc, part):
        gsend, _, blocks, with_nll = sums[part]
        base = gc * seg_groups
        out = pl.ds(pl.multiple_of(base, seg_groups), seg_groups)
        oh = (iota((seg_groups, tiles), 0) + base == grp_ref[...]).astype(F32).astype(BF16)
        oh = jnp.concatenate([oh, oh], axis=1)
        for b, m in enumerate(blocks):
            packed = None
            for j in range(0, pack, 2):
                at = (m * pack + j) * tiles
                rhs = jnp.concatenate(
                    [stacked(dmat[at:at + tiles]), stacked(dmat[at + tiles:at + 2 * tiles])], axis=1
                )
                both = jnp.dot(oh, rhs, preferred_element_type=F32)
                for h in range(2):
                    s = both[:, h * LANES:(h + 1) * LANES]
                    shift = LANES // 2
                    while shift >= quarter:
                        s = s + pltpu.roll(s, shift, 1)
                        shift //= 2
                    packed = s if packed is None else jnp.where(lane_g == j + h, s, packed)
            gsend[out, b * LANES:(b + 1) * LANES] = packed.astype(BF16)
        if with_nll:
            hi, lo = split(jnp.dot(oh, stacked(nll_ref[...]), preferred_element_type=F32))
            gsend[out, len(blocks) * LANES:] = (
                hi.astype(F32) + pltpu.roll(lo.astype(F32), chains, 1)
            ).astype(BF16)

    def g_copy(part, i):
        to = (me + i) % n
        return pltpu.make_async_remote_copy(
            src_ref=sums[part][0].at[pl.ds(pl.multiple_of(to * own, own), own)],
            dst_ref=sums[part][1].at[me], send_sem=g_ssem.at[part, i], recv_sem=g_rsem.at[part, i],
            device_id={"dp": to}, device_id_type=MESH,
        )

    for part in range(2):
        def run(gc, carry, part=part):
            segment(gc, part)
            return carry

        def start_g(i, carry, part=part):
            g_copy(part, i).start()
            return carry

        lax.fori_loop(0, groups // seg_groups, run, 0)
        lax.fori_loop(1, n, start_g, 0)
        sums[part][1][me] = sums[part][0][own_rows, :]

    def wait_g(i, carry):
        g_copy(0, i).wait()
        g_copy(1, i).wait()
        return carry

    lax.fori_loop(1, n, wait_g, 0)

    def add_g(i, total):
        return total[0] + grecv0[i].astype(F32), total[1] + grecv1[i].astype(F32)

    first, second = lax.fori_loop(0, n, add_g, (
        jnp.zeros((own, (cut + 1) * LANES), F32), jnp.zeros((own, (count - cut) * LANES), F32)
    ))
    lik_packed = jnp.concatenate([first[:, :cut * LANES], second], axis=1)
    parts = jnp.concatenate(split(lik_packed), axis=0)
    natural = nt_dot(parts, perm[...])
    lik = natural[:own] + natural[own:]
    mean, prec, mass = mean_ref[...], par_ref[0:1, :], par_ref[1:2, :]
    offset = newpos_ref[...] - mean
    new_gradient = lik + prec * offset
    new_momentum = half_ref[...] - 0.5 * step_size * new_gradient
    newgrad_ref[...] = new_gradient
    newmom_ref[...] = new_momentum
    out_grad = pltpu.make_async_copy(newgrad_ref, newgrad_out, out_sem.at[1])
    out_mom = pltpu.make_async_copy(newmom_ref, newmom_out, out_sem.at[2])
    out_grad.start()
    out_mom.start()
    quad = 0.5 * (prec * offset * offset + mass * new_momentum * new_momentum)
    q = quad[:, :LANES]
    for m in range(1, width // LANES):
        q = q + quad[:, m * LANES:(m + 1) * LANES]
    shift = LANES // 2
    while shift >= chains:
        q = q + pltpu.roll(q, shift, 1)
        shift //= 2
    loss = first[:, cut * LANES:]
    loss = loss + pltpu.roll(loss, LANES - chains, 1)
    esend[...] = q + loss

    def e_copy(i):
        return pltpu.make_async_remote_copy(
            src_ref=esend, dst_ref=erecv.at[feat], send_sem=e_ssem.at[i],
            recv_sem=e_rsem.at[i], device_id={"feat": (feat + i) % nf}, device_id_type=MESH,
        )

    for i in range(1, nf):
        e_copy(i).start()
    erecv[feat] = esend[...]
    for i in range(1, nf):
        e_copy(i).wait()
    e = erecv[0]
    for i in range(1, nf):
        e = e + erecv[i]
    energy_ref[...] = e[:, :chains]
    out_energy = pltpu.make_async_copy(energy_ref, energy_out, out_sem.at[3])
    out_energy.start()
    for f in (out_pos, out_grad, out_mom, out_energy):
        f.wait()


def finish(*refs):
    for a, b in zip(refs[:4], refs[4:]):
        b[...] = a[...]


def body(observations, labels, tile_live, tile_group, position, momentum, gradient, prior_mean, prior_prec, inv_mass):
    n, nf = lax.axis_size("dp"), lax.axis_size("feat")
    tiles, quarter, row_count = observations.shape
    own, width = position.shape
    chains = width // quarter
    pack = LANES // quarter
    half_rows = tiles * chains // 2
    anywhere = pl.BlockSpec(memory_space=pl.ANY)
    cut = width // LANES // 2 * LANES
    dma = pltpu.SemaphoreType.DMA
    block = jax.ShapeDtypeStruct((own, width), F32)
    results = pl.pallas_call(
        functools.partial(kernel, n, nf, chains, quarter),
        out_shape=(block, block, block, jax.ShapeDtypeStruct((own, chains), F32)),
        in_specs=[anywhere] * 10,
        out_specs=(anywhere,) * 4,
        scratch_shapes=[
            pltpu.VMEM((tiles, row_count), jnp.int32),
            pltpu.VMEM((1, tiles), jnp.int32),
            pltpu.VMEM((1, tiles), jnp.int32),
            pltpu.VMEM((own, width), F32),
            pltpu.VMEM((own, width), F32),
            pltpu.VMEM((own, width), F32),
            pltpu.VMEM((1, width), F32),
            pltpu.VMEM((2, quarter), F32),
            pltpu.VMEM((tiles, row_count), F32),
            pltpu.VMEM((2, width), F32),
            pltpu.VMEM((own, width), F32),
            pltpu.VMEM((own, width), F32),
            pltpu.VMEM((own, width), F32),
            pltpu.VMEM((own, chains), F32),
            pltpu.VMEM((tiles // pack, LANES, row_count), BF16),
            pltpu.VMEM((width, width), BF16),
            pltpu.VMEM((own, width), BF16),
            pltpu.VMEM((n * own, width), BF16),
            pltpu.VMEM((own, width), F32),
            pltpu.VMEM((tiles * chains, LANES), F32),
            pltpu.VMEM((half_rows, row_count), F32),
            pltpu.VMEM((half_rows, row_count), F32),
            pltpu.VMEM((half_rows, row_count), F32),
            pltpu.VMEM((half_rows, row_count), BF16),
            pltpu.VMEM((half_rows, row_count), BF16),
            pltpu.VMEM((half_rows, row_count), BF16),
            pltpu.VMEM((half_rows, row_count), BF16),
            pltpu.VMEM((tiles, LANES), F32),
            pltpu.VMEM((chains * tiles, LANES), F32),
            pltpu.VMEM((n * own, cut + LANES), BF16),
            pltpu.VMEM((n * own, width - cut), BF16),
            pltpu.VMEM((n, own, cut + LANES), BF16),
            pltpu.VMEM((n, own, width - cut), BF16),
            pltpu.VMEM((own, LANES), F32),
            pltpu.VMEM((nf, own, LANES), F32),
            dma((10,)), dma((4,)),
            dma((n,)), dma((n,)),
            dma((CHUNKS,)), dma((CHUNKS,)),
            dma((CHUNKS,)), dma((CHUNKS,)),
            dma((CHUNKS,)), dma((CHUNKS,)),
            dma((2, n)), dma((2, n)),
            dma((nf,)), dma((nf,)),
        ],
        compiler_params=pltpu.CompilerParams(collective_id=0, has_side_effects=True),
    )(
        observations.reshape(tiles // pack, LANES, row_count),
        labels, tile_live.reshape(1, tiles), tile_group.reshape(1, tiles),
        position, momentum, gradient,
        prior_mean.reshape(1, width), prior_prec.reshape(1, quarter), inv_mass.reshape(1, quarter),
    )
    return tuple(pl.pallas_call(
        finish,
        out_shape=tuple(jax.ShapeDtypeStruct(x.shape, x.dtype) for x in results),
        in_specs=[pl.BlockSpec(memory_space=pltpu.VMEM)] * 4,
        out_specs=(pl.BlockSpec(memory_space=pltpu.VMEM),) * 4,
    )(*results))


def solution(mesh):
    placed = (
        P("dp", "feat", None),
        P("dp", None),
        P("dp"),
        P("dp"),
        P("dp", "feat"),
        P("dp", "feat"),
        P("dp", "feat"),
        P("feat"),
        P("feat"),
        P("feat"),
    )
    return jax.shard_map(
        body,
        mesh=mesh,
        in_specs=placed,
        out_specs=(P("dp", "feat"), P("dp", "feat"), P("dp", "feat"), P("dp", None)),
        check_vma=False,
    )
```

profile of v0, /device:TPU:0, one launch (start us, length us, event | category | flops | bytes accessed | tf_op | source)
XLA Modules:
  0.0 35.3 jit_solution(3239636204944900163)
XLA Ops:
  0.6 33.2 %shard_map.129 = (f32[16,512]{1,0:T(8,128)}, f32[16,512]{1,0:T(8,128)}, f32[16,512]{1,0:T(8,128)}, f32[16,16]{1,0:T(8,128)}) custom-call(bf16[32,128,128]{2,1,0:T(8,128)(2,1)} %bitcast.6, s32[128,128]{1,0:T(8,128)} %lab_hbm.1, s32[1,128]{1,0:T(1,128)} %bitcast.8, s32[1,128]{1,0:T(1,128)} %bitcast.9, f32[16,512]{1,0:T(8,128)} %pos_hbm.1, f32[16,512]{1,0:T(8,128)} %mom_hbm.1, ...), custom_call_target="tpu_custom_call" | custom-call | tf_op jit(solution)/shard_map/pallas_call | solution.py:366
  33.8 1.4 %shard_map.130 = (f32[16,512]{1,0:T(8,128)}, f32[16,512]{1,0:T(8,128)}, f32[16,512]{1,0:T(8,128)}, f32[16,16]{1,0:T(8,128)}) custom-call(f32[16,512]{1,0:T(8,128)} %get-tuple-element.8.refs_0_, f32[16,512]{1,0:T(8,128)} %get-tuple-element.9.refs_1_, f32[16,512]{1,0:T(8,128)} %get-tuple-element.10.refs_2_, f32[16,16]{1,0:T(8,128)} %get-tuple-element.11.refs_3_), custom_call_target="tpu_custom_call" | custom-call | tf_op jit(solution)/shard_map/pallas_call | solution.py:422
where the time goes:
time: 35.5 us; the launch traced here: 35.3 us
  Pallas kernels  34.6 us (97%)
  between operations  0.64 us (2%)
    pallas_call x1, Pallas kernels, body(): pl.pallas_call(functools.partial(kernel, n, nf, chains, quarter), out_sha...  33.2 us
    pallas_call x1, Pallas kernels, body(): pl.pallas_call(finish, out_shape=tuple((jax.ShapeDtypeStruct(x.shape, x.d...  1.44 us

commit v1 on v0

v1 whole, which is shorter than its diff:
```python
import functools
import jax
import jax.numpy as jnp
from jax import lax
from jax.experimental import pallas as pl
from jax.experimental.pallas import tpu as pltpu
from jax.sharding import PartitionSpec as P

step_size = 0.1
LANES = 128
PARTS = 2
CHUNKS = 4
MESH = pl.DeviceIdType.MESH
BF16 = jnp.bfloat16
F32 = jnp.float32


def iota(shape, dim):
    return lax.broadcasted_iota(jnp.int32, shape, dim)


def split(x):
    hi = x.astype(BF16)
    return hi, (x - hi.astype(F32)).astype(BF16)


def nt_dot(a, b):
    return lax.dot_general(a, b, (((1,), (1,)), ((), ())), preferred_element_type=F32)


def kernel(
    n, nf, chains, quarter,
    obs_hbm, lab_hbm, live_hbm, grp_hbm, pos_hbm, mom_hbm, grad_hbm, mean_hbm, prec_hbm, mass_hbm,
    newpos_ref, newmom_ref, newgrad_ref, energy_ref,
    lab_in, live_ref, grp_ref, pos_ref, mom_ref, grad_ref, mean_ref, pair_ref,
    lab_ref, par_ref, obs, perm, wall, half_ref, hot_ref, lhs, mine, pair_send, pair_recv,
    far_send, far_recv, res_own, res_recv, nll_ref, dmat, gsend0, gsend1, grecv0, grecv1, esend, erecv,
    in_sem, w_ssem, w_rsem, p_ssem, p_rsem, f_ssem, f_rsem, r_ssem, r_rsem,
    g_ssem, g_rsem, e_ssem, e_rsem,
):
    me = lax.axis_index("dp")
    feat = lax.axis_index("feat")
    tiles = lab_ref.shape[0]
    own, width = pos_ref.shape
    pack = LANES // quarter
    part_chains = chains // PARTS
    part_width = width // PARTS
    quads = tiles // pack
    qrows = pack * part_chains
    half_quads = quads // 2
    chunk_quads = half_quads // CHUNKS
    chunk_tiles = chunk_quads * pack
    crows = chunk_quads * qrows
    groups = n * own
    bit = feat % 2
    near = feat + 1 - 2 * bit
    far = (feat + nf // 2) % nf

    rails = 2 - n % 2
    levels = n // rails
    level, rail = me // rails, me % rails
    mate = me + 1 - 2 * rail
    first_greeted = jnp.maximum(level - 1, 0) * rails
    heard = jnp.minimum((level + 2) * rails, n)

    sources = [
        (mass_hbm, pair_ref.at[1:2]), (prec_hbm, pair_ref.at[0:1]),
        (mom_hbm, mom_ref), (grad_hbm, grad_ref), (pos_hbm, pos_ref), (mean_hbm, mean_ref),
        (grp_hbm, grp_ref), (live_hbm, live_ref), (lab_hbm, lab_in), (obs_hbm, obs),
    ]
    fetches = [pltpu.make_async_copy(a, b, in_sem.at[i]) for i, (a, b) in enumerate(sources)]
    for f in fetches:
        f.start()

    barrier = pltpu.get_barrier_semaphore()

    def greet(i, carry):
        d = first_greeted + i
        d = d + (d >= me).astype(jnp.int32)
        pl.semaphore_signal(barrier, inc=1, device_id={"dp": d}, device_id_type=MESH)
        return carry

    lax.fori_loop(0, n - 1 - first_greeted, greet, 0)
    for i in range(1, nf):
        pl.semaphore_signal(barrier, inc=1, device_id={"feat": (feat + i) % nf}, device_id_type=MESH)

    spread = (iota((quarter, width), 0) == iota((quarter, width), 1) // chains).astype(F32)
    r, c = iota((width, width), 0), iota((width, width), 1)
    perm[...] = jnp.where(
        (r % chains == c // quarter) & (r // chains == c % quarter), 1.0, 0.0
    ).astype(BF16)
    for f in fetches[:5]:
        f.wait()
    par_ref[...] = jnp.dot(
        pair_ref[...], spread, precision=lax.Precision.HIGHEST, preferred_element_type=F32
    )
    half = mom_ref[...] - 0.5 * step_size * grad_ref[...]
    half_ref[...] = half
    moved = pos_ref[...] + step_size * par_ref[1:2, :] * half
    newpos_ref[...] = moved
    coeff = jnp.dot(moved.astype(BF16), perm[...], preferred_element_type=F32).astype(BF16)

    def block(d):
        return pl.ds(pl.multiple_of(d * own, own), own)

    for h in range(PARTS):
        wall[h, block(me), :] = coeff[:, h * part_width:(h + 1) * part_width]
    pl.semaphore_wait(barrier, heard - 1 + nf - 1)

    def w_copy(h, kind, at, origin, to):
        return pltpu.make_async_remote_copy(
            src_ref=wall.at[h, block(origin)], dst_ref=wall.at[h, block(origin)],
            send_sem=w_ssem.at[h, kind, at], recv_sem=w_rsem.at[h, origin],
            device_id={"dp": to}, device_id_type=MESH,
        )

    def ups(h, origin):
        out = [w_copy(h, 1, origin, origin, me + rails)]
        if rails > 1:
            out.append(w_copy(h, 2, origin, origin, mate + rails))
        return out

    has_up = level < levels - 1

    def send_up(h, origin):
        @pl.when(has_up)
        def _():
            for w in ups(h, origin):
                w.start()

    for h in range(PARTS):
        send_up(h, me)
        if rails > 1:
            w_copy(h, 0, mate, me, mate).start()

        def send_down(d, carry, h=h):
            w_copy(h, 0, d, me, d).start()
            return carry

        lax.fori_loop(0, level * rails, send_down, 0)

    square = iota((tiles, tiles), 0) == iota((tiles, tiles), 1)

    def column(row):
        return jnp.sum(jnp.where(square, row.astype(F32), 0.0), axis=1, keepdims=True)

    for f in fetches[5:9]:
        f.wait()
    hot_ref[...] = (
        iota((tiles, groups), 1).astype(F32) == column(grp_ref[...])
    ).astype(F32).astype(BF16)
    lab_ref[...] = jnp.where(
        iota(lab_ref.shape, 1).astype(F32) < column(live_ref[...]), lab_in[...].astype(F32), -1.0
    )
    nll_ref[...] = jnp.zeros_like(nll_ref)
    fetches[9].wait()

    def relay(i, carry):
        origin = me - (i + 1) * rails
        for h in range(PARTS):
            w_copy(h, 0, me, origin, mate).wait_recv()
            send_up(h, origin)
        return carry

    lax.fori_loop(0, level, relay, 0)

    row_t, lane_t = iota((tiles, LANES), 0), iota((tiles, LANES), 1)
    place = row_t % pack
    keep = lane_t // quarter == place

    def wait_blocks(h):
        def step(d, carry):
            relayed = (d // rails < level) & (d % rails == rail)

            @pl.when((d != me) & jnp.logical_not(relayed))
            def _():
                w_copy(h, 0, me, d, mate).wait_recv()
            return carry

        lax.fori_loop(0, n, step, 0)

    def pick(h):
        picked = jnp.dot(hot_ref[...], wall[h], preferred_element_type=F32)
        for m in range(part_width // LANES):
            x = picked[:, m * LANES:(m + 1) * LANES]
            turned = [x] + [pltpu.roll(x, s * quarter, 1) for s in range(1, pack)]
            for j in range(pack):
                y = turned[0]
                for s in range(1, pack):
                    y = jnp.where((place + pack - j) % pack == s, turned[s], y)
                lhs[pl.ds(h * tiles * part_chains + m * pack + j, tiles, stride=part_chains), :] = (
                    jnp.where(keep, y, 0.0)
                )

    def logits(h, first_quad, dst, base):
        for i in range(chunk_quads):
            q = first_quad + i
            at = h * tiles * part_chains + q * qrows
            a = lhs[pl.ds(pl.multiple_of(at, qrows), qrows), :].astype(BF16)
            dst[pl.ds(pl.multiple_of(base + i * qrows, qrows), qrows), :] = jnp.dot(
                a, obs[q], preferred_element_type=F32
            )

    def rows(u):
        return pl.ds(pl.multiple_of(u * crows, crows), crows)

    def pair_copy(u):
        return pltpu.make_async_remote_copy(
            src_ref=pair_send.at[rows(u)], dst_ref=pair_recv.at[rows(u)],
            send_sem=p_ssem.at[u], recv_sem=p_rsem.at[u],
            device_id={"feat": near}, device_id_type=MESH,
        )

    def far_copy(u):
        return pltpu.make_async_remote_copy(
            src_ref=far_send.at[rows(u)], dst_ref=far_recv.at[rows(u)],
            send_sem=f_ssem.at[u], recv_sem=f_rsem.at[u],
            device_id={"feat": far}, device_id_type=MESH,
        )

    def res_copy(u):
        return pltpu.make_async_remote_copy(
            src_ref=res_own.at[rows(u)], dst_ref=res_recv.at[rows(u)],
            send_sem=r_ssem.at[u], recv_sem=r_rsem.at[u],
            device_id={"feat": near}, device_id_type=MESH,
        )

    def stage_a(h, k):
        u = h * CHUNKS + k
        logits(h, (1 - bit) * half_quads + k * chunk_quads, pair_send, u * crows)
        pair_copy(u).start()
        logits(h, bit * half_quads + k * chunk_quads, mine, u * crows)

    def stage_b(h, k):
        u = h * CHUNKS + k
        pair_copy(u).wait()
        total = mine[rows(u), :] + pair_recv[rows(u), :]
        mine[rows(u), :] = total
        far_send[rows(u), :] = total.astype(BF16)
        far_copy(u).start()

    def loop(first, body):
        def step(k, carry):
            body(k)
            return carry

        lax.fori_loop(first, CHUNKS, step, 0)

    for h in range(PARTS):
        wait_blocks(h)
        pick(h)
        loop(0, lambda k: stage_a(h, k))
        loop(0, lambda k: stage_b(h, k))

    diag = iota((qrows, LANES), 0) // part_chains == iota((qrows, LANES), 1) // quarter

    def grads(h, first_quad, src, base):
        for i in range(chunk_quads):
            q = first_quad + i
            a = src[pl.ds(pl.multiple_of(base + i * qrows, qrows), qrows), :]
            g = jnp.where(diag, nt_dot(a, obs[q]), 0.0)
            for j in range(pack):
                dmat[pl.ds(h * part_chains * tiles + q * pack + j, part_chains, stride=tiles), :] = (
                    g[j * part_chains:(j + 1) * part_chains]
                )

    def stage_c(h, k):
        u = h * CHUNKS + k
        far_copy(u).wait()
        z = mine[rows(u), :] + far_recv[rows(u), :].astype(F32)
        first = pl.multiple_of((bit * half_quads + k * chunk_quads) * pack, chunk_tiles)
        lab = lab_ref[pl.ds(first, chunk_tiles), :]
        lab = jnp.broadcast_to(lab[:, None, :], (chunk_tiles, part_chains, LANES)).reshape(crows, LANES)
        live = lab >= 0.0
        e = jnp.exp(-jnp.abs(z))
        inv = 1.0 / (1.0 + e)
        sig = jnp.where(z >= 0.0, inv, e * inv)
        res_own[rows(u), :] = jnp.where(live, sig - lab, 0.0).astype(BF16)
        res_copy(u).start()
        v = jnp.where(live, jnp.maximum(z, 0.0) + jnp.log1p(e) - lab * z, 0.0)
        s = jnp.sum(v, axis=1, keepdims=True) * (2.0 / nf)
        at = iota((crows, LANES), 0) % part_chains + h * part_chains == iota((crows, LANES), 1)
        s = jnp.where(at, s, 0.0).reshape(chunk_tiles, part_chains, LANES)
        nll_ref[pl.ds(first, chunk_tiles), :] += jnp.sum(s, axis=1)
        grads(h, bit * half_quads + k * chunk_quads, res_own, u * crows)

    def stage_d(h, k):
        u = h * CHUNKS + k
        res_copy(u).wait()
        grads(h, (1 - bit) * half_quads + k * chunk_quads, res_recv, u * crows)

    def stage_cd(h, k):
        stage_c(h, k)
        stage_d(h, k - 1)

    seg_groups = min(groups, LANES)
    lane_g = iota((seg_groups, LANES), 1) // quarter
    blocks = part_width // LANES
    sums = ((gsend0, grecv0), (gsend1, grecv1))

    def stacked(d):
        return jnp.concatenate(split(d), axis=0)

    def segment(gc, h):
        gsend = sums[h][0]
        base = gc * seg_groups
        out = pl.ds(pl.multiple_of(base, seg_groups), seg_groups)
        oh = (iota((seg_groups, tiles), 0) + base == grp_ref[...]).astype(F32).astype(BF16)
        oh = jnp.concatenate([oh, oh], axis=1)
        for m in range(blocks):
            packed = None
            for j in range(0, pack, 2):
                at = (h * part_chains + m * pack + j) * tiles
                rhs = jnp.concatenate(
                    [stacked(dmat[at:at + tiles]), stacked(dmat[at + tiles:at + 2 * tiles])], axis=1
                )
                both = jnp.dot(oh, rhs, preferred_element_type=F32)
                for i in range(2):
                    s = both[:, i * LANES:(i + 1) * LANES]
                    shift = LANES // 2
                    while shift >= quarter:
                        s = s + pltpu.roll(s, shift, 1)
                        shift //= 2
                    packed = s if packed is None else jnp.where(lane_g == j + i, s, packed)
            gsend[out, m * LANES:(m + 1) * LANES] = packed.astype(BF16)
        if h == PARTS - 1:
            hi, lo = split(jnp.dot(oh, stacked(nll_ref[...]), preferred_element_type=F32))
            gsend[out, blocks * LANES:] = (
                hi.astype(F32) + pltpu.roll(lo.astype(F32), chains, 1)
            ).astype(BF16)

    def g_copy(h, to):
        return pltpu.make_async_remote_copy(
            src_ref=sums[h][0].at[block(to)], dst_ref=sums[h][1].at[me],
            send_sem=g_ssem.at[h, to], recv_sem=g_rsem.at[h, me],
            device_id={"dp": to}, device_id_type=MESH,
        )

    def g_from(h, d):
        return pltpu.make_async_remote_copy(
            src_ref=sums[h][0].at[block(d)], dst_ref=sums[h][1].at[d],
            send_sem=g_ssem.at[h, d], recv_sem=g_rsem.at[h, d],
            device_id={"dp": d}, device_id_type=MESH,
        )

    def others(body):
        def step(i, carry):
            body(i + (i >= me).astype(jnp.int32))
            return carry

        lax.fori_loop(0, n - 1, step, 0)

    def send_sums(h):
        def run(gc, carry):
            segment(gc, h)
            return carry

        lax.fori_loop(0, groups // seg_groups, run, 0)
        others(lambda d: g_copy(h, d).start())
        sums[h][1][me] = sums[h][0][block(me), :]

    stage_c(0, 0)
    loop(1, lambda k: stage_cd(0, k))
    for h in range(1, PARTS):
        stage_c(h, 0)
        stage_d(h - 1, CHUNKS - 1)
        send_sums(h - 1)
        loop(1, lambda k: stage_cd(h, k))
    stage_d(PARTS - 1, CHUNKS - 1)
    send_sums(PARTS - 1)

    def total_of(h):
        others(lambda d: g_from(h, d).wait())
        shape = sums[h][1].shape[1:]
        return lax.fori_loop(
            0, n, lambda i, t: t + sums[h][1][i].astype(F32), jnp.zeros(shape, F32)
        )

    def natural(packed, h):
        parts = jnp.concatenate(split(packed), axis=0)
        both = nt_dot(parts, perm[:, h * part_width:(h + 1) * part_width])
        return both[:own] + both[own:]

    def drain(h):
        @pl.when(has_up)
        def _():
            for w in ups(h, me):
                w.wait_send()

            def step(i, carry):
                for w in ups(h, me - (i + 1) * rails):
                    w.wait_send()
                return carry

            lax.fori_loop(0, level, step, 0)

        if rails > 1:
            w_copy(h, 0, mate, me, mate).wait_send()

        def down(d, carry):
            w_copy(h, 0, d, me, d).wait_send()
            return carry

        lax.fori_loop(0, level * rails, down, 0)

    for h in range(PARTS):
        drain(h)
    mean, prec, mass = mean_ref[...], par_ref[0:1, :], par_ref[1:2, :]
    offset = newpos_ref[...] - mean
    lik = prec * offset
    for h in range(PARTS):
        total = total_of(h)
        lik = lik + natural(total[:, :part_width], h)
    loss = total[:, part_width:]
    new_gradient = lik
    new_momentum = half_ref[...] - 0.5 * step_size * new_gradient
    newgrad_ref[...] = new_gradient
    newmom_ref[...] = new_momentum
    quad = 0.5 * (prec * offset * offset + mass * new_momentum * new_momentum)
    q = quad[:, :LANES]
    for m in range(1, width // LANES):
        q = q + quad[:, m * LANES:(m + 1) * LANES]
    shift = LANES // 2
    while shift >= chains:
        q = q + pltpu.roll(q, shift, 1)
        shift //= 2
    loss = loss + pltpu.roll(loss, LANES - chains, 1)
    esend[...] = q + loss

    def e_copy(i):
        return pltpu.make_async_remote_copy(
            src_ref=esend, dst_ref=erecv.at[feat], send_sem=e_ssem.at[i],
            recv_sem=e_rsem.at[i], device_id={"feat": (feat + i) % nf}, device_id_type=MESH,
        )

    for i in range(1, nf):
        e_copy(i).start()
    erecv[feat] = esend[...]
    for i in range(1, nf):
        e_copy(i).wait()
    e = erecv[0]
    for i in range(1, nf):
        e = e + erecv[i]
    energy_ref[...] = e[:, :chains]


def finish(*refs):
    sem = refs[8]
    copies = [pltpu.make_async_copy(refs[i], refs[4 + i], sem.at[i]) for i in range(4)]
    for c in copies:
        c.start()
    for c in copies:
        c.wait()


def body(observations, labels, tile_live, tile_group, position, momentum, gradient, prior_mean, prior_prec, inv_mass):
    n, nf = lax.axis_size("dp"), lax.axis_size("feat")
    tiles, quarter, row_count = observations.shape
    own, width = position.shape
    chains = width // quarter
    pack = LANES // quarter
    half_rows = tiles * chains // 2
    anywhere = pl.BlockSpec(memory_space=pl.ANY)
    units = PARTS * CHUNKS
    dma = pltpu.SemaphoreType.DMA
    block = pltpu.VMEM((own, width), F32)
    results = pl.pallas_call(
        functools.partial(kernel, n, nf, chains, quarter),
        out_shape=(block, block, block, pltpu.VMEM((own, chains), F32)),
        in_specs=[anywhere] * 10,
        out_specs=(pl.BlockSpec(memory_space=pltpu.VMEM),) * 4,
        scratch_shapes=[
            pltpu.VMEM((tiles, row_count), jnp.int32),
            pltpu.VMEM((1, tiles), jnp.int32),
            pltpu.VMEM((1, tiles), jnp.int32),
            pltpu.VMEM((own, width), F32),
            pltpu.VMEM((own, width), F32),
            pltpu.VMEM((own, width), F32),
            pltpu.VMEM((1, width), F32),
            pltpu.VMEM((2, quarter), F32),
            pltpu.VMEM((tiles, row_count), F32),
            pltpu.VMEM((2, width), F32),
            pltpu.VMEM((tiles // pack, LANES, row_count), BF16),
            pltpu.VMEM((width, width), BF16),
            pltpu.VMEM((PARTS, n * own, width // PARTS), BF16),
            pltpu.VMEM((own, width), F32),
            pltpu.VMEM((tiles, n * own), BF16),
            pltpu.VMEM((tiles * chains, LANES), F32),
            pltpu.VMEM((half_rows, row_count), F32),
            pltpu.VMEM((half_rows, row_count), F32),
            pltpu.VMEM((half_rows, row_count), F32),
            pltpu.VMEM((half_rows, row_count), BF16),
            pltpu.VMEM((half_rows, row_count), BF16),
            pltpu.VMEM((half_rows, row_count), BF16),
            pltpu.VMEM((half_rows, row_count), BF16),
            pltpu.VMEM((tiles, LANES), F32),
            pltpu.VMEM((chains * tiles, LANES), F32),
            pltpu.VMEM((n * own, width // PARTS), BF16),
            pltpu.VMEM((n * own, width // PARTS + LANES), BF16),
            pltpu.VMEM((n, own, width // PARTS), BF16),
            pltpu.VMEM((n, own, width // PARTS + LANES), BF16),
            pltpu.VMEM((own, LANES), F32),
            pltpu.VMEM((nf, own, LANES), F32),
            dma((10,)),
            dma((PARTS, 3, n)), dma((PARTS, n)),
            dma((units,)), dma((units,)),
            dma((units,)), dma((units,)),
            dma((units,)), dma((units,)),
            dma((PARTS, n)), dma((PARTS, n)),
            dma((nf,)), dma((nf,)),
        ],
        compiler_params=pltpu.CompilerParams(collective_id=0, has_side_effects=True),
    )(
        observations.reshape(tiles // pack, LANES, row_count),
        labels, tile_live.reshape(1, tiles), tile_group.reshape(1, tiles),
        position, momentum, gradient,
        prior_mean.reshape(1, width), prior_prec.reshape(1, quarter), inv_mass.reshape(1, quarter),
    )
    return tuple(pl.pallas_call(
        finish,
        out_shape=tuple(jax.ShapeDtypeStruct(x.shape, x.dtype) for x in results),
        in_specs=[pl.BlockSpec(memory_space=pltpu.VMEM)] * 4,
        out_specs=(anywhere,) * 4,
        scratch_shapes=[dma((4,))],
    )(*(pltpu.with_memory_space_constraint(x, pltpu.VMEM) for x in results)))


def solution(mesh):
    placed = (
        P("dp", "feat", None),
        P("dp", None),
        P("dp"),
        P("dp"),
        P("dp", "feat"),
        P("dp", "feat"),
        P("dp", "feat"),
        P("feat"),
        P("feat"),
        P("feat"),
    )
    return jax.shard_map(
        body,
        mesh=mesh,
        in_specs=placed,
        out_specs=(P("dp", "feat"), P("dp", "feat"), P("dp", "feat"), P("dp", None)),
        check_vma=False,
    )
```

time: 35.5 us -> 34.5 us (0.972)
  Pallas kernels: 34.6 us -> 33.7 us
    pallas_call x1, Pallas kernels: 1.44 us -> 0.68 us  [body(): pl.pallas_call(finish, out_shape=tuple((jax.ShapeDtypeStruct(x.shape, x.d...]
where the time goes in v1:
time: 34.5 us; the launch traced here: 34.4 us
  Pallas kernels  33.7 us (98%)
  between operations  0.64 us (2%)
    pallas_call x1, Pallas kernels, body(): pl.pallas_call(functools.partial(kernel, n, nf, chains, quarter), out_sha...  33 us

profile of v1, /device:TPU:0, one launch (start us, length us, event | category | flops | bytes accessed | tf_op | source)
XLA Modules:
  0.0 34.4 jit_solution(17162170078665955401)
XLA Ops:
  0.6 33.0 %shard_map.129 = (f32[16,512]{1,0:T(8,128)S(1)}, f32[16,512]{1,0:T(8,128)S(1)}, f32[16,512]{1,0:T(8,128)S(1)}, f32[16,16]{1,0:T(8,128)S(1)}) custom-call(bf16[32,128,128]{2,1,0:T(8,128)(2,1)} %bitcast.6, s32[128,128]{1,0:T(8,128)} %lab_hbm.1, s32[1,128]{1,0:T(1,128)} %bitcast.8, s32[1,128]{1,0:T(1,128)} %bitcast.9, f32[16,512]{1,0:T(8,128)} %pos_hbm.1, ...), custom_call_target="tpu_custom_call" | custom-call | tf_op jit(solution)/shard_map/pallas_call | solution.py:467
  33.7 0.7 %shard_map.130 = (f32[16,512]{1,0:T(8,128)}, f32[16,512]{1,0:T(8,128)}, f32[16,512]{1,0:T(8,128)}, f32[16,16]{1,0:T(8,128)}) custom-call(f32[16,512]{1,0:T(8,128)S(1)} %get-tuple-element.8.refs_0_, f32[16,512]{1,0:T(8,128)S(1)} %get-tuple-element.9.refs_1_, f32[16,512]{1,0:T(8,128)S(1)} %get-tuple-element.10.refs_2_, f32[16,16]{1,0:T(8,128)S(1)} %get-tuple-element.11.refs_3_), custom_call_target="tpu_custom_call" | custom-call | tf_op jit(solution)/shard_map/pallas_call | solution.py:519

commit v2 on v1

v2 whole, which is shorter than its diff:
```python
import functools
import jax
import jax.numpy as jnp
from jax import lax
from jax.experimental import pallas as pl
from jax.experimental.pallas import tpu as pltpu
from jax.sharding import PartitionSpec as P

step_size = 0.1
LANES = 128
PARTS = 2
CHUNKS = 4
MESH = pl.DeviceIdType.MESH
BF16 = jnp.bfloat16
F32 = jnp.float32


def iota(shape, dim):
    return lax.broadcasted_iota(jnp.int32, shape, dim)


def split(x):
    hi = x.astype(BF16)
    return hi, (x - hi.astype(F32)).astype(BF16)


def nt_dot(a, b):
    return lax.dot_general(a, b, (((1,), (1,)), ((), ())), preferred_element_type=F32)


def kernel(
    n, nf, chains, quarter,
    obs_hbm, lab_hbm, live_hbm, grp_hbm, pos_hbm, mom_hbm, grad_hbm, mean_hbm, prec_hbm, mass_hbm,
    newpos_ref, newmom_ref, newgrad_ref, energy_ref,
    lab_in, live_ref, grp_ref, pos_ref, mom_ref, grad_ref, mean_ref, pair_ref,
    lab_ref, par_ref, obs, perm, wall, half_ref, hot_ref, sum_ref, lhs, mine, pair_send, pair_recv,
    far_send, far_recv, res_own, res_recv, nll_ref, dmat, acc, gsend0, gsend1, grecv0, grecv1, esend, erecv,
    in_sem, w_ssem, w_rsem, p_ssem, p_rsem, f_ssem, f_rsem, r_ssem, r_rsem,
    g_ssem, g_rsem, e_ssem, e_rsem,
):
    me = lax.axis_index("dp")
    feat = lax.axis_index("feat")
    tiles = lab_ref.shape[0]
    own, width = pos_ref.shape
    pack = LANES // quarter
    part_chains = chains // PARTS
    part_width = width // PARTS
    quads = tiles // pack
    qrows = pack * part_chains
    half_quads = quads // 2
    chunk_quads = half_quads // CHUNKS
    chunk_tiles = chunk_quads * pack
    crows = chunk_quads * qrows
    groups = n * own
    bit = feat % 2
    near = feat + 1 - 2 * bit
    far = (feat + nf // 2) % nf

    barrier = pltpu.get_barrier_semaphore()

    def others(body):
        def up(i, carry):
            body(n - 1 - i)
            return carry

        def down(d, carry):
            body(d)
            return carry

        lax.fori_loop(0, n - 1 - me, up, 0)
        lax.fori_loop(0, me, down, 0)

    def greet(d):
        pl.semaphore_signal(barrier, inc=1, device_id={"dp": d}, device_id_type=MESH)

    others(greet)
    for i in range(1, nf):
        pl.semaphore_signal(barrier, inc=1, device_id={"feat": (feat + i) % nf}, device_id_type=MESH)

    sources = [
        (mass_hbm, pair_ref.at[1:2]), (prec_hbm, pair_ref.at[0:1]),
        (mom_hbm, mom_ref), (grad_hbm, grad_ref), (pos_hbm, pos_ref), (mean_hbm, mean_ref),
        (grp_hbm, grp_ref), (live_hbm, live_ref), (lab_hbm, lab_in), (obs_hbm, obs),
    ]
    fetches = [pltpu.make_async_copy(a, b, in_sem.at[i]) for i, (a, b) in enumerate(sources)]
    for f in fetches:
        f.start()

    spread = (iota((quarter, width), 0) == iota((quarter, width), 1) // chains).astype(F32)
    r, c = iota((width, width), 0), iota((width, width), 1)
    perm[...] = jnp.where(
        (r % chains == c // quarter) & (r // chains == c % quarter), 1.0, 0.0
    ).astype(BF16)
    for f in fetches[:5]:
        f.wait()
    par_ref[...] = jnp.dot(
        pair_ref[...], spread, precision=lax.Precision.HIGHEST, preferred_element_type=F32
    )
    half = mom_ref[...] - 0.5 * step_size * grad_ref[...]
    half_ref[...] = half
    moved = pos_ref[...] + step_size * par_ref[1:2, :] * half
    newpos_ref[...] = moved
    coeff = jnp.dot(moved.astype(BF16), perm[...], preferred_element_type=F32).astype(BF16)

    def block(d):
        return pl.ds(pl.multiple_of(d * own, own), own)

    for h in range(PARTS):
        wall[h, block(me), :] = coeff[:, h * part_width:(h + 1) * part_width]
    pl.semaphore_wait(barrier, n - 1 + nf - 1)

    def w_copy(h, to):
        return pltpu.make_async_remote_copy(
            src_ref=wall.at[h, block(me)], dst_ref=wall.at[h, block(me)],
            send_sem=w_ssem.at[h], recv_sem=w_rsem.at[h],
            device_id={"dp": to}, device_id_type=MESH,
        )

    def w_all(h):
        blocks = wall.at[h, pl.ds(0, (n - 1) * own)]
        return pltpu.make_async_remote_copy(
            src_ref=blocks, dst_ref=blocks, send_sem=w_ssem.at[h], recv_sem=w_rsem.at[h],
            device_id={"dp": (me + 1) % n}, device_id_type=MESH,
        )

    for h in range(PARTS):
        others(lambda d: w_copy(h, d).start())

    square = iota((tiles, tiles), 0) == iota((tiles, tiles), 1)

    def column(row):
        return jnp.sum(jnp.where(square, row.astype(F32), 0.0), axis=1, keepdims=True)

    for f in fetches[5:9]:
        f.wait()
    hot_ref[...] = (
        iota((tiles, groups), 1).astype(F32) == column(grp_ref[...])
    ).astype(F32).astype(BF16)
    member = (iota((groups, tiles), 0) == grp_ref[...]).astype(F32).astype(BF16)
    for i in range(2):
        side = member[:, i * (tiles // 2):(i + 1) * (tiles // 2)]
        sum_ref[i] = jnp.concatenate([side, side], axis=1)
    lab_ref[...] = jnp.where(
        iota(lab_ref.shape, 1).astype(F32) < column(live_ref[...]), lab_in[...].astype(F32), -1.0
    )
    nll_ref[...] = jnp.zeros_like(nll_ref)
    fetches[9].wait()

    half_tiles = tiles // 2
    row_t, lane_t = iota((half_tiles, LANES), 0), iota((half_tiles, LANES), 1)
    place = row_t % pack
    keep = lane_t // quarter == place
    mine_first, near_first = bit * half_tiles, (1 - bit) * half_tiles

    def pick(h, first):
        picked = jnp.dot(
            hot_ref[pl.ds(pl.multiple_of(first, half_tiles), half_tiles), :], wall[h],
            preferred_element_type=F32,
        )
        for m in range(part_width // LANES):
            x = picked[:, m * LANES:(m + 1) * LANES]
            turned = [x] + [pltpu.roll(x, s * quarter, 1) for s in range(1, pack)]
            for j in range(pack):
                y = turned[0]
                for s in range(1, pack):
                    y = jnp.where((place + pack - j) % pack == s, turned[s], y)
                at = (h * tiles + first) * part_chains + m * pack + j
                lhs[pl.ds(at, half_tiles, stride=part_chains), :] = jnp.where(keep, y, 0.0)

    def logits(h, first_quad, dst, base):
        for i in range(chunk_quads):
            q = first_quad + i
            at = h * tiles * part_chains + q * qrows
            a = lhs[pl.ds(pl.multiple_of(at, qrows), qrows), :].astype(BF16)
            dst[base + i * qrows:base + (i + 1) * qrows, :] = jnp.dot(
                a, obs[q], preferred_element_type=F32
            ).astype(dst.dtype)

    units = PARTS * CHUNKS

    def rows(u):
        return pl.ds(u * crows, crows)

    def exchange(src, dst, ssem, rsem, to):
        def copy(u):
            return pltpu.make_async_remote_copy(
                src_ref=src.at[rows(u)], dst_ref=dst.at[rows(u)], send_sem=ssem.at[0],
                recv_sem=rsem.at[u], device_id={"feat": to}, device_id_type=MESH,
            )

        def drain():
            pltpu.make_async_remote_copy(
                src_ref=src, dst_ref=dst, send_sem=ssem.at[0], recv_sem=rsem.at[0],
                device_id={"feat": to}, device_id_type=MESH,
            ).wait_send()

        return copy, drain

    pair_copy, pair_drain = exchange(pair_send, pair_recv, p_ssem, p_rsem, near)
    far_copy, far_drain = exchange(far_send, far_recv, f_ssem, f_rsem, far)
    res_copy, res_drain = exchange(res_own, res_recv, r_ssem, r_rsem, near)

    for h in range(PARTS):
        w_all(h).wait_recv()
        pick(h, near_first)
        for k in range(CHUNKS):
            u = h * CHUNKS + k
            logits(h, (1 - bit) * half_quads + k * chunk_quads, pair_send, u * crows)
            pair_copy(u).start()
        pick(h, mine_first)
        for k in range(CHUNKS):
            u = h * CHUNKS + k
            logits(h, bit * half_quads + k * chunk_quads, mine, u * crows)
        for k in range(CHUNKS):
            u = h * CHUNKS + k
            pair_copy(u).wait_recv()
            total = mine[rows(u), :] + pair_recv[rows(u), :].astype(F32)
            mine[rows(u), :] = total
            far_send[rows(u), :] = total.astype(BF16)
            far_copy(u).start()

    diag = iota((qrows, LANES), 0) // part_chains == iota((qrows, LANES), 1) // quarter

    def grads(h, first_quad, src, base):
        for i in range(chunk_quads):
            q = first_quad + i
            g = jnp.where(diag, nt_dot(src[base + i * qrows:base + (i + 1) * qrows, :], obs[q]), 0.0)
            for j in range(pack):
                dmat[pl.ds(h * part_chains * tiles + q * pack + j, part_chains, stride=tiles), :] = (
                    g[j * part_chains:(j + 1) * part_chains]
                )

    def stage_c(h, k):
        u = h * CHUNKS + k
        far_copy(u).wait_recv()
        z = mine[rows(u), :] + far_recv[rows(u), :].astype(F32)
        first = pl.multiple_of((bit * half_quads + k * chunk_quads) * pack, chunk_tiles)
        lab = lab_ref[pl.ds(first, chunk_tiles), :]
        lab = jnp.broadcast_to(lab[:, None, :], (chunk_tiles, part_chains, LANES)).reshape(crows, LANES)
        live = lab >= 0.0
        e = jnp.exp(-jnp.abs(z))
        inv = 1.0 / (1.0 + e)
        sig = jnp.where(z >= 0.0, inv, e * inv)
        res_own[rows(u), :] = jnp.where(live, sig - lab, 0.0).astype(BF16)
        res_copy(u).start()
        v = jnp.where(live, jnp.maximum(z, 0.0) + jnp.log(1.0 + e) - lab * z, 0.0)
        s = jnp.sum(v, axis=1, keepdims=True) * (2.0 / nf)
        at = iota((crows, LANES), 0) % part_chains + h * part_chains == iota((crows, LANES), 1)
        s = jnp.where(at, s, 0.0).reshape(chunk_tiles, part_chains, LANES)
        nll_ref[pl.ds(first, chunk_tiles), :] += jnp.sum(s, axis=1)
        grads(h, bit * half_quads + k * chunk_quads, res_own, u * crows)

    def stage_d(h, k):
        u = h * CHUNKS + k
        res_copy(u).wait_recv()
        grads(h, (1 - bit) * half_quads + k * chunk_quads, res_recv, u * crows)

    seg_groups = min(groups, LANES)
    lane_g = iota((seg_groups, LANES), 1) // quarter
    blocks = part_width // LANES
    sums = ((gsend0, grecv0), (gsend1, grecv1))

    def stacked(d):
        return jnp.concatenate(split(d), axis=0)

    def segment(gc, h, first, last):
        gsend = sums[h][0]
        base = gc * seg_groups
        out = pl.ds(pl.multiple_of(base, seg_groups), seg_groups)
        oh = sum_ref[first // half_tiles, out, :]
        for m in range(blocks):
            packed = None
            for j in range(0, pack, 2):
                pair = []
                for i in range(2):
                    at = (h * part_chains + m * pack + j + i) * tiles + first
                    pair.append(stacked(dmat[pl.ds(pl.multiple_of(at, half_tiles), half_tiles), :]))
                both = jnp.dot(oh, jnp.concatenate(pair, axis=1), preferred_element_type=F32)
                for i in range(2):
                    s = both[:, i * LANES:(i + 1) * LANES]
                    shift = LANES // 2
                    while shift >= quarter:
                        s = s + pltpu.roll(s, shift, 1)
                        shift //= 2
                    packed = s if packed is None else jnp.where(lane_g == j + i, s, packed)
            cols = slice(m * LANES, (m + 1) * LANES)
            if last:
                gsend[out, cols] = (acc[out, cols] + packed).astype(BF16)
            else:
                acc[out, cols] = packed
        if h == PARTS - 1 and not last:
            mine_nll = nll_ref[pl.ds(pl.multiple_of(first, half_tiles), half_tiles), :]
            hi, lo = split(jnp.dot(oh, stacked(mine_nll), preferred_element_type=F32))
            gsend[out, blocks * LANES:] = (
                hi.astype(F32) + pltpu.roll(lo.astype(F32), chains, 1)
            ).astype(BF16)

    def add_half(h, first, last):
        def run(gc, carry):
            segment(gc, h, first, last)
            return carry

        lax.fori_loop(0, groups // seg_groups, run, 0)

    def g_copy(h, to):
        return pltpu.make_async_remote_copy(
            src_ref=sums[h][0].at[block(to)], dst_ref=sums[h][1].at[me],
            send_sem=g_ssem.at[h], recv_sem=g_rsem.at[h],
            device_id={"dp": to}, device_id_type=MESH,
        )

    def g_all(h):
        return pltpu.make_async_remote_copy(
            src_ref=sums[h][1].at[pl.ds(0, n - 1)], dst_ref=sums[h][1].at[pl.ds(0, n - 1)],
            send_sem=g_ssem.at[h], recv_sem=g_rsem.at[h],
            device_id={"dp": (me + 1) % n}, device_id_type=MESH,
        )

    def send_sums(h):
        others(lambda d: g_copy(h, d).start())
        sums[h][1][me] = sums[h][0][block(me), :]

    for h in range(PARTS):
        for k in range(CHUNKS):
            stage_c(h, k)
            if k:
                stage_d(h, k - 1)
            elif h:
                stage_d(h - 1, CHUNKS - 1)
                add_half(h - 1, near_first, True)
                send_sums(h - 1)
        add_half(h, mine_first, False)
    stage_d(PARTS - 1, CHUNKS - 1)
    add_half(PARTS - 1, near_first, True)
    send_sums(PARTS - 1)

    def total_of(h):
        g_all(h).wait_recv()
        shape = sums[h][1].shape[1:]
        return lax.fori_loop(
            0, n, lambda i, t: t + sums[h][1][i].astype(F32), jnp.zeros(shape, F32)
        )

    def natural(packed, h):
        parts = jnp.concatenate(split(packed), axis=0)
        both = nt_dot(parts, perm[:, h * part_width:(h + 1) * part_width])
        return both[:own] + both[own:]

    mean, prec, mass = mean_ref[...], par_ref[0:1, :], par_ref[1:2, :]
    offset = newpos_ref[...] - mean
    lik = prec * offset
    for h in range(PARTS):
        total = total_of(h)
        lik = lik + natural(total[:, :part_width], h)
    loss = total[:, part_width:]
    new_gradient = lik
    new_momentum = half_ref[...] - 0.5 * step_size * new_gradient
    newgrad_ref[...] = new_gradient
    newmom_ref[...] = new_momentum
    quad = 0.5 * (prec * offset * offset + mass * new_momentum * new_momentum)
    q = quad[:, :LANES]
    for m in range(1, width // LANES):
        q = q + quad[:, m * LANES:(m + 1) * LANES]
    shift = LANES // 2
    while shift >= chains:
        q = q + pltpu.roll(q, shift, 1)
        shift //= 2
    loss = loss + pltpu.roll(loss, LANES - chains, 1)
    esend[...] = q + loss

    def e_copy(i):
        return pltpu.make_async_remote_copy(
            src_ref=esend, dst_ref=erecv.at[feat], send_sem=e_ssem.at[0],
            recv_sem=e_rsem.at[0], device_id={"feat": (feat + i) % nf}, device_id_type=MESH,
        )

    for i in range(1, nf):
        e_copy(i).start()
    erecv[feat] = esend[...]
    for drain in (pair_drain, far_drain, res_drain):
        drain()
    for h in range(PARTS):
        w_all(h).wait_send()
        g_all(h).wait_send()
    pltpu.make_async_remote_copy(
        src_ref=erecv.at[pl.ds(0, nf - 1)], dst_ref=erecv.at[pl.ds(0, nf - 1)],
        send_sem=e_ssem.at[0], recv_sem=e_rsem.at[0],
        device_id={"feat": near}, device_id_type=MESH,
    ).wait()
    e = erecv[0]
    for i in range(1, nf):
        e = e + erecv[i]
    energy_ref[...] = e[:, :chains]


def finish(*refs):
    sem = refs[8]
    copies = [pltpu.make_async_copy(refs[i], refs[4 + i], sem.at[i]) for i in range(4)]
    for c in copies:
        c.start()
    for c in copies:
        c.wait()


def body(observations, labels, tile_live, tile_group, position, momentum, gradient, prior_mean, prior_prec, inv_mass):
    n, nf = lax.axis_size("dp"), lax.axis_size("feat")
    tiles, quarter, row_count = observations.shape
    own, width = position.shape
    chains = width // quarter
    pack = LANES // quarter
    half_rows = tiles * chains // 2
    anywhere = pl.BlockSpec(memory_space=pl.ANY)
    units = PARTS * CHUNKS
    dma = pltpu.SemaphoreType.DMA
    block = pltpu.VMEM((own, width), F32)
    results = pl.pallas_call(
        functools.partial(kernel, n, nf, chains, quarter),
        out_shape=(block, block, block, pltpu.VMEM((own, chains), F32)),
        in_specs=[anywhere] * 10,
        out_specs=(pl.BlockSpec(memory_space=pltpu.VMEM),) * 4,
        scratch_shapes=[
            pltpu.VMEM((tiles, row_count), jnp.int32),
            pltpu.VMEM((1, tiles), jnp.int32),
            pltpu.VMEM((1, tiles), jnp.int32),
            pltpu.VMEM((own, width), F32),
            pltpu.VMEM((own, width), F32),
            pltpu.VMEM((own, width), F32),
            pltpu.VMEM((1, width), F32),
            pltpu.VMEM((2, quarter), F32),
            pltpu.VMEM((tiles, row_count), F32),
            pltpu.VMEM((2, width), F32),
            pltpu.VMEM((tiles // pack, LANES, row_count), BF16),
            pltpu.VMEM((width, width), BF16),
            pltpu.VMEM((PARTS, n * own, width // PARTS), BF16),
            pltpu.VMEM((own, width), F32),
            pltpu.VMEM((tiles, n * own), BF16),
            pltpu.VMEM((2, n * own, tiles), BF16),
            pltpu.VMEM((tiles * chains, LANES), F32),
            pltpu.VMEM((half_rows, row_count), F32),
            pltpu.VMEM((half_rows, row_count), F32),
            pltpu.VMEM((half_rows, row_count), F32),
            pltpu.VMEM((half_rows, row_count), BF16),
            pltpu.VMEM((half_rows, row_count), BF16),
            pltpu.VMEM((half_rows, row_count), BF16),
            pltpu.VMEM((half_rows, row_count), BF16),
            pltpu.VMEM((tiles, LANES), F32),
            pltpu.VMEM((chains * tiles, LANES), F32),
            pltpu.VMEM((n * own, width // PARTS), F32),
            pltpu.VMEM((n * own, width // PARTS), BF16),
            pltpu.VMEM((n * own, width // PARTS + LANES), BF16),
            pltpu.VMEM((n, own, width // PARTS), BF16),
            pltpu.VMEM((n, own, width // PARTS + LANES), BF16),
            pltpu.VMEM((own, LANES), F32),
            pltpu.VMEM((nf, own, LANES), F32),
            dma((10,)),
            dma((PARTS,)), dma((PARTS,)),
            dma((1,)), dma((units,)),
            dma((1,)), dma((units,)),
            dma((1,)), dma((units,)),
            dma((PARTS,)), dma((PARTS,)),
            dma((1,)), dma((1,)),
        ],
        compiler_params=pltpu.CompilerParams(collective_id=0, has_side_effects=True),
    )(
        observations.reshape(tiles // pack, LANES, row_count),
        labels, tile_live.reshape(1, tiles), tile_group.reshape(1, tiles),
        position, momentum, gradient,
        prior_mean.reshape(1, width), prior_prec.reshape(1, quarter), inv_mass.reshape(1, quarter),
    )
    return tuple(pl.pallas_call(
        finish,
        out_shape=tuple(jax.ShapeDtypeStruct(x.shape, x.dtype) for x in results),
        in_specs=[pl.BlockSpec(memory_space=pltpu.VMEM)] * 4,
        out_specs=(anywhere,) * 4,
        scratch_shapes=[dma((4,))],
    )(*(pltpu.with_memory_space_constraint(x, pltpu.VMEM) for x in results)))


def solution(mesh):
    placed = (
        P("dp", "feat", None),
        P("dp", None),
        P("dp"),
        P("dp"),
        P("dp", "feat"),
        P("dp", "feat"),
        P("dp", "feat"),
        P("feat"),
        P("feat"),
        P("feat"),
    )
    return jax.shard_map(
        body,
        mesh=mesh,
        in_specs=placed,
        out_specs=(P("dp", "feat"), P("dp", "feat"), P("dp", "feat"), P("dp", None)),
        check_vma=False,
    )
```

time: 34.5 us -> 30.7 us (0.89)
  Pallas kernels: 33.7 us -> 30 us
    pallas_call x1, Pallas kernels: 33 us -> 29.3 us  [body(): pl.pallas_call(functools.partial(kernel, n, nf, chains, quarter), out_sha...]
where the time goes in v2:
time: 30.7 us; the launch traced here: 30.6 us
  Pallas kernels  30 us (98%)
  between operations  0.64 us (2%)
    pallas_call x1, Pallas kernels, body(): pl.pallas_call(functools.partial(kernel, n, nf, chains, quarter), out_sha...  29.3 us
    pallas_call x1, Pallas kernels, body(): pl.pallas_call(finish, out_shape=tuple((jax.ShapeDtypeStruct(x.shape, x.d...  0.68 us

profile of v2, /device:TPU:0, one launch (start us, length us, event | category | flops | bytes accessed | tf_op | source)
XLA Modules:
  0.0 30.6 jit_solution(519452358041996574)
XLA Ops:
  0.6 29.3 %shard_map.129 = (f32[16,512]{1,0:T(8,128)S(1)}, f32[16,512]{1,0:T(8,128)S(1)}, f32[16,512]{1,0:T(8,128)S(1)}, f32[16,16]{1,0:T(8,128)S(1)}) custom-call(bf16[32,128,128]{2,1,0:T(8,128)(2,1)} %bitcast.6, s32[128,128]{1,0:T(8,128)} %lab_hbm.1, s32[1,128]{1,0:T(1,128)} %bitcast.8, s32[1,128]{1,0:T(1,128)} %bitcast.9, f32[16,512]{1,0:T(8,128)} %pos_hbm.1, ...), custom_call_target="tpu_custom_call" | custom-call | tf_op jit(solution)/shard_map/pallas_call | solution.py:416
  29.9 0.7 %shard_map.130 = (f32[16,512]{1,0:T(8,128)}, f32[16,512]{1,0:T(8,128)}, f32[16,512]{1,0:T(8,128)}, f32[16,16]{1,0:T(8,128)}) custom-call(f32[16,512]{1,0:T(8,128)S(1)} %get-tuple-element.8.refs_0_, f32[16,512]{1,0:T(8,128)S(1)} %get-tuple-element.9.refs_1_, f32[16,512]{1,0:T(8,128)S(1)} %get-tuple-element.10.refs_2_, f32[16,16]{1,0:T(8,128)S(1)} %get-tuple-element.11.refs_3_), custom_call_target="tpu_custom_call" | custom-call | tf_op jit(solution)/shard_map/pallas_call | solution.py:470

commit v3 on v2

v3 whole, which is shorter than its diff:
```python
import functools
import jax
import jax.numpy as jnp
from jax import lax
from jax.experimental import pallas as pl
from jax.experimental.pallas import tpu as pltpu
from jax.sharding import PartitionSpec as P

step_size = 0.1
LANES = 128
PARTS = 2
CHUNKS = 4
MESH = pl.DeviceIdType.MESH
BF16 = jnp.bfloat16
F32 = jnp.float32


def iota(shape, dim):
    return lax.broadcasted_iota(jnp.int32, shape, dim)


def split(x):
    hi = x.astype(BF16)
    return hi, (x - hi.astype(F32)).astype(BF16)


def nt_dot(a, b):
    return lax.dot_general(a, b, (((1,), (1,)), ((), ())), preferred_element_type=F32)


def kernel(
    n, nf, chains, quarter,
    obs_hbm, lab_hbm, live_hbm, grp_hbm, pos_hbm, mom_hbm, grad_hbm, mean_hbm, prec_hbm, mass_hbm,
    newpos_ref, newmom_ref, newgrad_ref, energy_ref,
    lab_in, live_ref, grp_ref, pos_ref, mom_ref, grad_ref, mean_ref, pair_ref,
    lab_ref, par_ref, obs, perm, back, hand, wall, half_ref, hot_ref, sum_ref, lhs, mine, pair_send, pair_recv,
    far_send, far_recv, res_own, res_recv, nll_ref, dmat, acc, gsend0, gsend1, grecv0, grecv1, esend, erecv,
    in_sem, h_ssem, h_rsem, w_ssem, w_rsem, t_sem, p_ssem, p_rsem, f_ssem, f_rsem, r_ssem, r_rsem,
    g_ssem, g_rsem, e_ssem, e_rsem,
):
    me = lax.axis_index("dp")
    feat = lax.axis_index("feat")
    tiles = lab_ref.shape[0]
    own, width = pos_ref.shape
    pack = LANES // quarter
    part_chains = chains // PARTS
    part_width = width // PARTS
    octet = 2 * pack
    orows = octet * part_chains
    half_octets = tiles // octet // 2
    chunk_octets = half_octets // CHUNKS
    chunk_tiles = chunk_octets * octet
    crows = chunk_octets * orows
    groups = n * own
    bit = feat % 2
    near = feat + 1 - 2 * bit
    far = (feat + nf // 2) % nf

    barrier = pltpu.get_barrier_semaphore()

    def above(body):
        def step(i, carry):
            body(n - 1 - i)
            return carry

        lax.fori_loop(0, n - 1 - me, step, 0)

    def below(body):
        def step(d, carry):
            body(d)
            return carry

        lax.fori_loop(0, me, step, 0)

    def others(body):
        above(body)
        below(body)

    def greet(d):
        pl.semaphore_signal(barrier, inc=1, device_id={"dp": d}, device_id_type=MESH)

    leads = bit == 1

    @pl.when(leads)
    def _():
        below(greet)

    above(greet)
    for i in range(1, nf):
        pl.semaphore_signal(barrier, inc=1, device_id={"feat": (feat + i) % nf}, device_id_type=MESH)

    sources = [
        (mass_hbm, pair_ref.at[1:2]), (prec_hbm, pair_ref.at[0:1]),
        (mom_hbm, mom_ref), (grad_hbm, grad_ref), (pos_hbm, pos_ref), (mean_hbm, mean_ref),
        (grp_hbm, grp_ref), (live_hbm, live_ref), (lab_hbm, lab_in), (obs_hbm, obs),
    ]
    fetches = [pltpu.make_async_copy(a, b, in_sem.at[i]) for i, (a, b) in enumerate(sources)]
    for f in fetches:
        f.start()

    spread = (iota((quarter, width), 0) == iota((quarter, width), 1) // chains).astype(F32)
    r, c = iota((width, width), 0), iota((width, width), 1)
    perm[...] = jnp.where(
        (r % chains == c // quarter) & (r // chains == c % quarter), 1.0, 0.0
    ).astype(BF16)
    for f in fetches[:5]:
        f.wait()
    par_ref[...] = jnp.dot(
        pair_ref[...], spread, precision=lax.Precision.HIGHEST, preferred_element_type=F32
    )
    half = mom_ref[...] - 0.5 * step_size * grad_ref[...]
    half_ref[...] = half
    moved = pos_ref[...] + step_size * par_ref[1:2, :] * half
    newpos_ref[...] = moved
    coeff = jnp.dot(moved.astype(BF16), perm[...], preferred_element_type=F32).astype(BF16)

    back[...] = jnp.where(
        (c % chains == r // quarter) & (c // chains == r % quarter), 1.0, 0.0
    ).astype(BF16)

    def block(d):
        return pl.ds(pl.multiple_of(d * own, own), own)

    for h in range(PARTS):
        hand[h] = coeff[:, h * part_width:(h + 1) * part_width]

    for h in range(PARTS):
        wall[0, h, block(me), :] = hand[h]
    pl.semaphore_wait(barrier, me + (n - 1 - me) * bit + nf - 1)

    def remote(src, dst, ssem, rsem, to):
        return pltpu.make_async_remote_copy(
            src_ref=src, dst_ref=dst, send_sem=ssem, recv_sem=rsem,
            device_id=to, device_id_type=MESH,
        )

    def hand_copy(h):
        return remote(
            hand.at[h], wall.at[1, h, block(me)], h_ssem.at[0], h_rsem.at[0], {"feat": near}
        )

    def w_copy(h, to, ssem):
        rows = wall.at[0, h, block(me)]
        return remote(rows, rows, ssem, w_rsem.at[h], {"dp": to})

    def t_copy(h, d, to):
        rows = wall.at[1, h, block(d)]
        return remote(rows, rows, w_ssem.at[1], t_sem.at[h, d], {"dp": to})

    def w_all(h):
        blocks = wall.at[0, h, pl.ds(0, (n - 1) * own)]
        return remote(blocks, blocks, w_ssem.at[0], w_rsem.at[h], {"dp": (me + 1) % n})

    def sent(side):
        blocks = wall.at[side, :, pl.ds(0, (n - 1) * own)]
        return remote(blocks, blocks, w_ssem.at[side], w_rsem.at[0], {"dp": (me + 1) % n})

    def pass_on(h, d):
        return remote(
            wall.at[1, h, block(d)], wall.at[0, h, block(d)], w_ssem.at[1], w_rsem.at[h],
            {"feat": near},
        )

    hand_all = remote(hand, hand, h_ssem.at[0], h_rsem.at[0], {"feat": near})

    @pl.when(jnp.logical_not(leads))
    def _():
        for h in range(PARTS):
            hand_copy(h).start()
        for h in range(PARTS):
            below(lambda d: w_copy(h, d, t_sem.at[h, d]).start())

    def send_both(h, d):
        t_copy(h, me, d).start()
        w_copy(h, d, w_ssem.at[0]).start()

    @pl.when(leads)
    def _():
        for h in range(PARTS):
            below(lambda d: w_copy(h, d, w_ssem.at[0]).start())
        hand_all.wait_recv()
        for h in range(PARTS):
            above(lambda d: send_both(h, d))

    square = iota((tiles, tiles), 0) == iota((tiles, tiles), 1)

    def column(row):
        return jnp.sum(jnp.where(square, row.astype(F32), 0.0), axis=1, keepdims=True)

    for f in fetches[5:9]:
        f.wait()
    hot_ref[...] = (
        iota((tiles, groups), 1).astype(F32) == column(grp_ref[...])
    ).astype(F32).astype(BF16)
    member = (iota((groups, tiles), 0) == grp_ref[...]).astype(F32).astype(BF16)
    for i in range(2):
        side = member[:, i * (tiles // 2):(i + 1) * (tiles // 2)]
        sum_ref[i] = jnp.concatenate([side, side], axis=1)
    lab_ref[...] = jnp.where(
        iota(lab_ref.shape, 1).astype(F32) < column(live_ref[...]), lab_in[...].astype(F32), -1.0
    )
    nll_ref[...] = jnp.zeros_like(nll_ref)
    fetches[9].wait()

    half_tiles = tiles // 2
    row_t, lane_t = iota((tiles, LANES), 0), iota((tiles, LANES), 1)
    place = row_t % pack
    keep = lane_t // quarter == place
    sides = (keep & (row_t % octet < pack), keep & (row_t % octet >= pack))
    mine_first, near_first = bit * half_tiles, (1 - bit) * half_tiles

    def hand_over(h, d):
        t_copy(h, d, d).wait_recv()
        pass_on(h, d).start()

    def relay(h):
        @pl.when(leads)
        def _():
            below(lambda d: hand_over(h, d))

    def pick(h):
        picked = jnp.dot(hot_ref[...], wall[0, h], preferred_element_type=F32)
        for m in range(part_width // LANES):
            x = picked[:, m * LANES:(m + 1) * LANES]
            turned = [x] + [pltpu.roll(x, s * quarter, 1) for s in range(1, pack)]
            spots = []
            for j in range(pack):
                y = turned[0]
                for s in range(1, pack):
                    y = jnp.where((place + pack - j) % pack == s, turned[s], y)
                spots.append(y)
            for j in range(0, pack, 2):
                at = (m * pack + j) * octet
                for i, side in enumerate(sides):
                    two = jnp.concatenate([
                        jnp.where(side, y, 0.0).reshape(tiles // octet, octet, LANES)
                        for y in spots[j:j + 2]
                    ], axis=1)
                    lhs[h, :, at:at + 2 * octet, i * LANES:(i + 1) * LANES] = two.astype(BF16)

    def logits(h, first_octet, dst, base):
        for i in range(chunk_octets):
            o = first_octet + i
            dst[base + i * orows:base + (i + 1) * orows, :] = jnp.dot(
                lhs[h, o], obs[o], preferred_element_type=F32
            ).astype(dst.dtype)

    units = PARTS * CHUNKS

    def rows(u):
        return pl.ds(u * crows, crows)

    def exchange(src, dst, ssem, rsem, to):
        def copy(u):
            at = pl.ds(u * crows, crows)
            return remote(src.at[at], dst.at[at], ssem.at[0], rsem.at[u], {"feat": to})

        def drain():
            pltpu.make_async_remote_copy(
                src_ref=src, dst_ref=dst, send_sem=ssem.at[0], recv_sem=rsem.at[0],
                device_id={"feat": to}, device_id_type=MESH,
            ).wait_send()

        return copy, drain

    pair_copy, pair_drain = exchange(pair_send, pair_recv, p_ssem, p_rsem, near)
    far_copy, far_drain = exchange(far_send, far_recv, f_ssem, f_rsem, far)
    res_copy, res_drain = exchange(res_own, res_recv, r_ssem, r_rsem, near)

    for h in range(PARTS):
        if h == 0:
            relay(h)

        w_all(h).wait_recv()
        pick(h)
        mark = h * CHUNKS
        for k in range(CHUNKS):
            logits(h, (1 - bit) * half_octets + k * chunk_octets, pair_send, (mark + k) * crows)
        for u in range(mark, mark + CHUNKS):
            pair_copy(u).start()
        if h + 1 < PARTS:
            relay(h + 1)
        for k in range(CHUNKS):
            logits(h, bit * half_octets + k * chunk_octets, mine, (mark + k) * crows)
        for u in range(mark, mark + CHUNKS):
            pair_copy(u).wait_recv()
            total = mine[rows(u), :] + pair_recv[rows(u), :].astype(F32)
            mine[rows(u), :] = total
            far_send[rows(u), :] = total.astype(BF16)
            far_copy(u).start()

    spot = iota((orows, LANES), 0) % octet
    diag = tuple(spot == iota((orows, LANES), 1) // quarter + i * pack for i in range(2))

    def grads(h, first_octet, src, base):
        for i in range(chunk_octets):
            o = first_octet + i
            g = nt_dot(src[base + i * orows:base + (i + 1) * orows, :], obs[o])
            g = jnp.where(diag[0], g[:, :LANES], jnp.where(diag[1], g[:, LANES:], 0.0))
            tile = pl.ds(pl.multiple_of(o * octet, octet), octet)
            dmat[h * part_chains:(h + 1) * part_chains, tile, :] = g.reshape(part_chains, octet, LANES)

    def residual(u):
        h, k = divmod(u, CHUNKS)
        z = mine[rows(u), :] + far_recv[rows(u), :].astype(F32)
        first = pl.multiple_of((bit * half_octets + k * chunk_octets) * octet, chunk_tiles)
        lab = lab_ref[pl.ds(first, chunk_tiles), :]
        lab = lab.reshape(chunk_octets, 1, octet, LANES)
        lab = jnp.broadcast_to(lab, (chunk_octets, part_chains, octet, LANES)).reshape(crows, LANES)
        live = lab >= 0.0
        e = jnp.exp(-jnp.abs(z))
        inv = 1.0 / (1.0 + e)
        sig = jnp.where(z >= 0.0, inv, e * inv)
        res_own[rows(u), :] = jnp.where(live, sig - lab, 0.0).astype(BF16)
        res_copy(u).start()
        v = jnp.where(live, jnp.maximum(z, 0.0) + jnp.log(1.0 + e) - lab * z, 0.0)
        s = jnp.sum(v, axis=1, keepdims=True) * (2.0 / nf)
        at = iota((crows, LANES), 0) // octet % part_chains + h * part_chains == iota((crows, LANES), 1)
        s = jnp.where(at, s, 0.0).reshape(chunk_octets, part_chains, octet, LANES)
        nll_ref[pl.ds(first, chunk_tiles), :] += jnp.sum(s, axis=1).reshape(chunk_tiles, LANES)

    def mine_grads(u):
        h, k = divmod(u, CHUNKS)
        grads(h, bit * half_octets + k * chunk_octets, res_own, u * crows)

    def near_grads(u):
        h, k = divmod(u, CHUNKS)
        grads(h, (1 - bit) * half_octets + k * chunk_octets, res_recv, u * crows)

    seg_groups = min(groups, LANES)
    lane_g = iota((half_tiles, LANES), 1) // quarter
    blocks = part_width // LANES
    sums = ((gsend0, grecv0), (gsend1, grecv1))

    def stacked(d):
        return jnp.concatenate(split(d), axis=0)

    def fold(xs, width):
        if len(xs) == 1:
            return xs[0]
        half = len(xs) // 2
        shift = half * width
        low = lane_g % len(xs) < half
        pairs = []
        for a, b in zip(xs[:half], xs[half:]):
            other = jnp.where(low, b, a)
            if len(xs) == pack:
                moved = pltpu.roll(other, shift, 1)
            else:
                moved = jnp.where(
                    low, pltpu.roll(other, LANES - shift, 1), pltpu.roll(other, shift, 1)
                )
            pairs.append(jnp.where(low, a, b) + moved)
        return fold(pairs, width)

    def compact(h, first):
        out = []
        for m in range(blocks):
            xs = []
            for j in range(pack):
                tile = pl.ds(pl.multiple_of(first, half_tiles), half_tiles)
                xs.append(dmat[h * part_chains + m * pack + j, tile, :])
            out.append(fold(xs, quarter))
        return stacked(jnp.concatenate(out, axis=1))

    def over_groups(body):
        def run(gc, carry):
            body(pl.ds(pl.multiple_of(gc * seg_groups, seg_groups), seg_groups))
            return carry

        if groups == seg_groups:
            body(pl.ds(0, groups))
        else:
            lax.fori_loop(0, groups // seg_groups, run, 0)

    def member_dot(side, out, rhs):
        return jnp.dot(sum_ref[side, out, :], rhs, preferred_element_type=F32)

    def start_half(h):
        rhs = compact(h, mine_first)
        nll = None
        if h == PARTS - 1:
            nll = stacked(nll_ref[pl.ds(pl.multiple_of(mine_first, half_tiles), half_tiles), :])

        def body(out):
            acc[out, :] = member_dot(bit, out, rhs)
            if nll is not None:
                hi, lo = split(member_dot(bit, out, nll))
                sums[h][0][out, part_width:] = (
                    hi.astype(F32) + pltpu.roll(lo.astype(F32), chains, 1)
                ).astype(BF16)

        over_groups(body)

    def whole(h):
        rhs = compact(h, mine_first), compact(h, near_first)

        def body(out):
            sums[h][0][out, :part_width] = (
                member_dot(bit, out, rhs[0]) + member_dot(1 - bit, out, rhs[1])
            ).astype(BF16)

        over_groups(body)

    def finish_half(h):
        rhs = compact(h, near_first)

        def body(out):
            sums[h][0][out, :part_width] = (acc[out, :] + member_dot(1 - bit, out, rhs)).astype(BF16)

        over_groups(body)

    def g_copy(h, to):
        return pltpu.make_async_remote_copy(
            src_ref=sums[h][0].at[block(to)], dst_ref=sums[h][1].at[me],
            send_sem=g_ssem.at[h], recv_sem=g_rsem.at[h],
            device_id={"dp": to}, device_id_type=MESH,
        )

    def g_all(h):
        return pltpu.make_async_remote_copy(
            src_ref=sums[h][1].at[pl.ds(0, n - 1)], dst_ref=sums[h][1].at[pl.ds(0, n - 1)],
            send_sem=g_ssem.at[h], recv_sem=g_rsem.at[h],
            device_id={"dp": (me + 1) % n}, device_id_type=MESH,
        )

    def send_sums(h):
        others(lambda d: g_copy(h, d).start())
        sums[h][1][me] = sums[h][0][block(me), :]

    lag = 2
    for u in range(units):
        far_copy(u).wait_recv()
        if u >= lag:
            res_copy(u - lag).wait_recv()
        residual(u)
        mine_grads(u)
        if u >= lag:
            near_grads(u - lag)
            h, k = divmod(u - lag, CHUNKS)
            if k == CHUNKS - 1:
                whole(h)
                send_sums(h)
    for u in range(units - lag, units - 1):
        res_copy(u).wait_recv()
        near_grads(u)
    start_half(PARTS - 1)
    res_copy(units - 1).wait_recv()
    near_grads(units - 1)
    finish_half(PARTS - 1)
    send_sums(PARTS - 1)

    def total_of(h):
        g_all(h).wait_recv()
        return jnp.sum(sums[h][1][...].astype(F32), axis=0)

    def natural(packed, h):
        parts = jnp.concatenate(split(packed), axis=0)
        both = jnp.dot(
            parts, back[h * part_width:(h + 1) * part_width, :], preferred_element_type=F32
        )
        return both[:own] + both[own:]

    mean, prec, mass = mean_ref[...], par_ref[0:1, :], par_ref[1:2, :]
    offset = newpos_ref[...] - mean
    lik = prec * offset
    for h in range(PARTS):
        total = total_of(h)
        lik = lik + natural(total[:, :part_width], h)
    loss = total[:, part_width:]
    new_gradient = lik
    new_momentum = half_ref[...] - 0.5 * step_size * new_gradient
    newgrad_ref[...] = new_gradient
    newmom_ref[...] = new_momentum
    quad = 0.5 * (prec * offset * offset + mass * new_momentum * new_momentum)
    q = quad[:, :LANES]
    for m in range(1, width // LANES):
        q = q + quad[:, m * LANES:(m + 1) * LANES]
    shift = LANES // 2
    while shift >= chains:
        q = q + pltpu.roll(q, shift, 1)
        shift //= 2
    loss = loss + pltpu.roll(loss, LANES - chains, 1)
    esend[...] = q + loss

    def e_copy(i):
        return pltpu.make_async_remote_copy(
            src_ref=esend, dst_ref=erecv.at[feat], send_sem=e_ssem.at[0],
            recv_sem=e_rsem.at[0], device_id={"feat": (feat + i) % nf}, device_id_type=MESH,
        )

    for i in range(1, nf):
        e_copy(i).start()
    erecv[feat] = esend[...]
    for drain in (pair_drain, far_drain, res_drain):
        drain()
    for h in range(PARTS):
        g_all(h).wait_send()

    @pl.when(leads)
    def _():
        for side in range(2):
            sent(side).wait_send()

    @pl.when(jnp.logical_not(leads))
    def _():
        hand_all.wait_send()
        for h in range(PARTS):
            below(lambda d: w_copy(h, d, t_sem.at[h, d]).wait_send())

    pltpu.make_async_remote_copy(
        src_ref=erecv.at[pl.ds(0, nf - 1)], dst_ref=erecv.at[pl.ds(0, nf - 1)],
        send_sem=e_ssem.at[0], recv_sem=e_rsem.at[0],
        device_id={"feat": near}, device_id_type=MESH,
    ).wait()
    e = erecv[0]
    for i in range(1, nf):
        e = e + erecv[i]
    energy_ref[...] = e[:, :chains]


def finish(*refs):
    sem = refs[8]
    copies = [pltpu.make_async_copy(refs[i], refs[4 + i], sem.at[i]) for i in range(4)]
    for c in copies:
        c.start()
    for c in copies:
        c.wait()


def body(observations, labels, tile_live, tile_group, position, momentum, gradient, prior_mean, prior_prec, inv_mass):
    n, nf = lax.axis_size("dp"), lax.axis_size("feat")
    tiles, quarter, row_count = observations.shape
    own, width = position.shape
    chains = width // quarter
    pack = LANES // quarter
    half_rows = tiles * chains // 2
    anywhere = pl.BlockSpec(memory_space=pl.ANY)
    units = PARTS * CHUNKS
    dma = pltpu.SemaphoreType.DMA
    block = pltpu.VMEM((own, width), F32)
    results = pl.pallas_call(
        functools.partial(kernel, n, nf, chains, quarter),
        out_shape=(block, block, block, pltpu.VMEM((own, chains), F32)),
        in_specs=[anywhere] * 10,
        out_specs=(pl.BlockSpec(memory_space=pltpu.VMEM),) * 4,
        scratch_shapes=[
            pltpu.VMEM((tiles, row_count), jnp.int32),
            pltpu.VMEM((1, tiles), jnp.int32),
            pltpu.VMEM((1, tiles), jnp.int32),
            pltpu.VMEM((own, width), F32),
            pltpu.VMEM((own, width), F32),
            pltpu.VMEM((own, width), F32),
            pltpu.VMEM((1, width), F32),
            pltpu.VMEM((2, quarter), F32),
            pltpu.VMEM((tiles, row_count), F32),
            pltpu.VMEM((2, width), F32),
            pltpu.VMEM((tiles // pack // 2, 2 * LANES, row_count), BF16),
            pltpu.VMEM((width, width), BF16),
            pltpu.VMEM((width, width), BF16),
            pltpu.VMEM((PARTS, own, width // PARTS), BF16),
            pltpu.VMEM((2, PARTS, n * own, width // PARTS), BF16),
            pltpu.VMEM((own, width), F32),
            pltpu.VMEM((tiles, n * own), BF16),
            pltpu.VMEM((2, n * own, tiles), BF16),
            pltpu.VMEM((PARTS, tiles // pack // 2, 2 * pack * chains // PARTS, 2 * LANES), BF16),
            pltpu.VMEM((half_rows, row_count), F32),
            pltpu.VMEM((half_rows, row_count), F32),
            pltpu.VMEM((half_rows, row_count), F32),
            pltpu.VMEM((half_rows, row_count), BF16),
            pltpu.VMEM((half_rows, row_count), BF16),
            pltpu.VMEM((half_rows, row_count), BF16),
            pltpu.VMEM((half_rows, row_count), BF16),
            pltpu.VMEM((tiles, LANES), F32),
            pltpu.VMEM((chains, tiles, LANES), F32),
            pltpu.VMEM((n * own, width // PARTS), F32),
            pltpu.VMEM((n * own, width // PARTS), BF16),
            pltpu.VMEM((n * own, width // PARTS + LANES), BF16),
            pltpu.VMEM((n, own, width // PARTS), BF16),
            pltpu.VMEM((n, own, width // PARTS + LANES), BF16),
            pltpu.VMEM((own, LANES), F32),
            pltpu.VMEM((nf, own, LANES), F32),
            dma((10,)),
            dma((1,)), dma((1,)),
            dma((2,)), dma((PARTS,)), dma((PARTS, n)),
            dma((1,)), dma((units,)),
            dma((1,)), dma((units,)),
            dma((1,)), dma((units,)),
            dma((PARTS,)), dma((PARTS,)),
            dma((1,)), dma((1,)),
        ],
        compiler_params=pltpu.CompilerParams(collective_id=0, has_side_effects=True),
    )(
        observations.reshape(tiles // pack // 2, 2 * LANES, row_count),
        labels, tile_live.reshape(1, tiles), tile_group.reshape(1, tiles),
        position, momentum, gradient,
        prior_mean.reshape(1, width), prior_prec.reshape(1, quarter), inv_mass.reshape(1, quarter),
    )
    return tuple(pl.pallas_call(
        finish,
        out_shape=tuple(jax.ShapeDtypeStruct(x.shape, x.dtype) for x in results),
        in_specs=[pl.BlockSpec(memory_space=pltpu.VMEM)] * 4,
        out_specs=(anywhere,) * 4,
        scratch_shapes=[dma((4,))],
    )(*(pltpu.with_memory_space_constraint(x, pltpu.VMEM) for x in results)))


def solution(mesh):
    placed = (
        P("dp", "feat", None),
        P("dp", None),
        P("dp"),
        P("dp"),
        P("dp", "feat"),
        P("dp", "feat"),
        P("dp", "feat"),
        P("feat"),
        P("feat"),
        P("feat"),
    )
    return jax.shard_map(
        body,
        mesh=mesh,
        in_specs=placed,
        out_specs=(P("dp", "feat"), P("dp", "feat"), P("dp", "feat"), P("dp", None)),
        check_vma=False,
    )
```

time: 30.7 us -> 29.2 us (0.951)
  Pallas kernels: 30 us -> 28.4 us
    pallas_call x1, Pallas kernels: 29.3 us -> 27.7 us  [body(): pl.pallas_call(functools.partial(kernel, n, nf, chains, quarter), out_sha...]
where the time goes in v3:
time: 29.2 us; the launch traced here: 29 us
  Pallas kernels  28.4 us (97%)
  between operations  0.64 us (2%)
    pallas_call x1, Pallas kernels, body(): pl.pallas_call(functools.partial(kernel, n, nf, chains, quarter), out_sha...  27.7 us
    pallas_call x1, Pallas kernels, body(): pl.pallas_call(finish, out_shape=tuple((jax.ShapeDtypeStruct(x.shape, x.d...  0.68 us

profile of v3, /device:TPU:0, one launch (start us, length us, event | category | flops | bytes accessed | tf_op | source)
XLA Modules:
  0.0 29.0 jit_solution(14640664939130108204)
XLA Ops:
  0.6 27.7 %shard_map.129 = (f32[16,512]{1,0:T(8,128)S(1)}, f32[16,512]{1,0:T(8,128)S(1)}, f32[16,512]{1,0:T(8,128)S(1)}, f32[16,16]{1,0:T(8,128)S(1)}) custom-call(bf16[16,256,128]{2,1,0:T(8,128)(2,1)} %bitcast.6, s32[128,128]{1,0:T(8,128)} %lab_hbm.1, s32[1,128]{1,0:T(1,128)} %bitcast.8, s32[1,128]{1,0:T(1,128)} %bitcast.9, f32[16,512]{1,0:T(8,128)} %pos_hbm.1, ...), custom_call_target="tpu_custom_call" | custom-call | tf_op jit(solution)/shard_map/pallas_call | solution.py:542
  28.4 0.7 %shard_map.130 = (f32[16,512]{1,0:T(8,128)}, f32[16,512]{1,0:T(8,128)}, f32[16,512]{1,0:T(8,128)}, f32[16,16]{1,0:T(8,128)}) custom-call(f32[16,512]{1,0:T(8,128)S(1)} %get-tuple-element.8.refs_0_, f32[16,512]{1,0:T(8,128)S(1)} %get-tuple-element.9.refs_1_, f32[16,512]{1,0:T(8,128)S(1)} %get-tuple-element.10.refs_2_, f32[16,16]{1,0:T(8,128)S(1)} %get-tuple-element.11.refs_3_), custom_call_target="tpu_custom_call" | custom-call | tf_op jit(solution)/shard_map/pallas_call | solution.py:599

commit v4 on v3

--- a/solution.py
+++ b/solution.py
@@ -33,11 +33,13 @@
     obs_hbm, lab_hbm, live_hbm, grp_hbm, pos_hbm, mom_hbm, grad_hbm, mean_hbm, prec_hbm, mass_hbm,
     newpos_ref, newmom_ref, newgrad_ref, energy_ref,
     lab_in, live_ref, grp_ref, pos_ref, mom_ref, grad_ref, mean_ref, pair_ref,
-    lab_ref, par_ref, obs, perm, back, hand, wall, half_ref, hot_ref, sum_ref, lhs, mine, pair_send, pair_recv,
-    far_send, far_recv, res_own, res_recv, nll_ref, dmat, acc, gsend0, gsend1, grecv0, grecv1, esend, erecv,
-    in_sem, h_ssem, h_rsem, w_ssem, w_rsem, t_sem, p_ssem, p_rsem, f_ssem, f_rsem, r_ssem, r_rsem,
-    g_ssem, g_rsem, e_ssem, e_rsem,
+    lab_ref, par_ref, obs, perm, back, hand, wall, half_ref, drift_ref, lane_mass_ref, gather_ref, e0_ref, hot_ref, sum_ref, lhs, mine, pair_send, pair_recv,
+    far_send, far_recv, res_own, res_recv, nll_ref, dmat, acc, gsend0, gsend1, nsend, grecv0, grecv1, nrecv, esend, erecv,
+    in_sem, h_rsem, w_rsem, t_sem, p_rsem, f_rsem, g_rsem, e_rsem,
 ):
+    h_ssem, w_ssem, p_ssem, f_ssem = (in_sem.at[i:j] for i, j in ((0, 1), (1, 3), (3, 4), (4, 5)))
+    r_ssem, g_ssem, e_ssem = (in_sem.at[i:j] for i, j in ((5, 6), (6, 9), (9, 10)))
+    r_rsem = t_sem.at[0]
     me = lax.axis_index("dp")
     feat = lax.axis_index("feat")
     tiles = lab_ref.shape[0]
@@ -200,6 +202,31 @@
         iota(lab_ref.shape, 1).astype(F32) < column(live_ref[...]), lab_in[...].astype(F32), -1.0
     )
     nll_ref[...] = jnp.zeros_like(nll_ref)
+    offset = newpos_ref[...] - mean_ref[...]
+    force = par_ref[0:1, :] * offset
+    drift = half_ref[...] - 0.5 * step_size * force
+    high, rest = split(drift)
+    low = (drift - high.astype(F32) - rest.astype(F32)).astype(BF16)
+    packed = jnp.dot(
+        jnp.concatenate([high, rest, low], axis=0), perm[...], preferred_element_type=F32
+    )
+    drift_ref[...] = packed[:own] + packed[own:2 * own] + packed[2 * own:]
+    lane_mass_ref[...] = jnp.dot(
+        pair_ref[...], (iota((quarter, width), 0) == iota((quarter, width), 1) % quarter).astype(F32),
+        precision=lax.Precision.HIGHEST, preferred_element_type=F32,
+    )[1:2, :]
+    gather_ref[...] = (
+        iota((width, LANES), 0) // quarter == iota((width, LANES), 1)
+    ).astype(F32).astype(BF16)
+    prior = 0.5 * force * offset
+    e0 = prior[:, :LANES]
+    for m in range(1, width // LANES):
+        e0 = e0 + prior[:, m * LANES:(m + 1) * LANES]
+    shift = LANES // 2
+    while shift >= chains:
+        e0 = e0 + pltpu.roll(e0, shift, 1)
+        shift //= 2
+    e0_ref[...] = e0
     fetches[9].wait()
 
     half_tiles = tiles // 2
@@ -272,6 +299,9 @@
             relay(h)
 
         w_all(h).wait_recv()
+        pl.when(jnp.logical_not(leads))(
+            lambda: below(lambda d: w_copy(h, d, t_sem.at[h, d]).wait_send())
+        )
         pick(h)
         mark = h * CHUNKS
         for k in range(CHUNKS):
@@ -330,7 +360,7 @@
     seg_groups = min(groups, LANES)
     lane_g = iota((half_tiles, LANES), 1) // quarter
     blocks = part_width // LANES
-    sums = ((gsend0, grecv0), (gsend1, grecv1))
+    sums = ((gsend0, grecv0), (gsend1, grecv1), (nsend, nrecv))
 
     def stacked(d):
         return jnp.concatenate(split(d), axis=0)
@@ -386,7 +416,7 @@
             acc[out, :] = member_dot(bit, out, rhs)
             if nll is not None:
                 hi, lo = split(member_dot(bit, out, nll))
-                sums[h][0][out, part_width:] = (
+                nsend[out, :] = (
                     hi.astype(F32) + pltpu.roll(lo.astype(F32), chains, 1)
                 ).astype(BF16)
 
@@ -396,7 +426,7 @@
         rhs = compact(h, mine_first), compact(h, near_first)
 
         def body(out):
-            sums[h][0][out, :part_width] = (
+            sums[h][0][out, :] = (
                 member_dot(bit, out, rhs[0]) + member_dot(1 - bit, out, rhs[1])
             ).astype(BF16)
 
@@ -406,7 +436,7 @@
         rhs = compact(h, near_first)
 
         def body(out):
-            sums[h][0][out, :part_width] = (acc[out, :] + member_dot(1 - bit, out, rhs)).astype(BF16)
+            sums[h][0][out, :] = (acc[out, :] + member_dot(1 - bit, out, rhs)).astype(BF16)
 
         over_groups(body)
 
@@ -445,6 +475,7 @@
         res_copy(u).wait_recv()
         near_grads(u)
     start_half(PARTS - 1)
+    send_sums(PARTS)
     res_copy(units - 1).wait_recv()
     near_grads(units - 1)
     finish_half(PARTS - 1)
@@ -461,27 +492,19 @@
         )
         return both[:own] + both[own:]
 
-    mean, prec, mass = mean_ref[...], par_ref[0:1, :], par_ref[1:2, :]
-    offset = newpos_ref[...] - mean
-    lik = prec * offset
+    energy = e0_ref[...]
+    totals = []
     for h in range(PARTS):
-        total = total_of(h)
-        lik = lik + natural(total[:, :part_width], h)
-    loss = total[:, part_width:]
-    new_gradient = lik
-    new_momentum = half_ref[...] - 0.5 * step_size * new_gradient
-    newgrad_ref[...] = new_gradient
-    newmom_ref[...] = new_momentum
-    quad = 0.5 * (prec * offset * offset + mass * new_momentum * new_momentum)
-    q = quad[:, :LANES]
-    for m in range(1, width // LANES):
-        q = q + quad[:, m * LANES:(m + 1) * LANES]
-    shift = LANES // 2
-    while shift >= chains:
-        q = q + pltpu.roll(q, shift, 1)
-        shift //= 2
-    loss = loss + pltpu.roll(loss, LANES - chains, 1)
-    esend[...] = q + loss
+        if h == PARTS - 1:
+            loss = total_of(PARTS)
+            energy = energy + loss + pltpu.roll(loss, LANES - chains, 1)
+        totals.append(total_of(h))
+        cols = slice(h * part_width, (h + 1) * part_width)
+        t = drift_ref[:, cols] - 0.5 * step_size * totals[h]
+        parts = stacked(0.5 * lane_mass_ref[:, cols] * t * t)
+        both = jnp.dot(parts, gather_ref[cols, :], preferred_element_type=F32)
+        energy = energy + both[:own] + both[own:]
+    esend[...] = energy
 
     def e_copy(i):
         return pltpu.make_async_remote_copy(
@@ -492,9 +515,14 @@
     for i in range(1, nf):
         e_copy(i).start()
     erecv[feat] = esend[...]
+    new_gradient = par_ref[0:1, :] * (newpos_ref[...] - mean_ref[...])
+    for h in range(PARTS):
+        new_gradient = new_gradient + natural(totals[h], h)
+    newgrad_ref[...] = new_gradient
+    newmom_ref[...] = half_ref[...] - 0.5 * step_size * new_gradient
     for drain in (pair_drain, far_drain, res_drain):
         drain()
-    for h in range(PARTS):
+    for h in range(PARTS + 1):
         g_all(h).wait_send()
 
     @pl.when(leads)
@@ -505,8 +533,6 @@
     @pl.when(jnp.logical_not(leads))
     def _():
         hand_all.wait_send()
-        for h in range(PARTS):
-            below(lambda d: w_copy(h, d, t_sem.at[h, d]).wait_send())
 
     pltpu.make_async_remote_copy(
         src_ref=erecv.at[pl.ds(0, nf - 1)], dst_ref=erecv.at[pl.ds(0, nf - 1)],
@@ -561,6 +587,10 @@
             pltpu.VMEM((PARTS, own, width // PARTS), BF16),
             pltpu.VMEM((2, PARTS, n * own, width // PARTS), BF16),
             pltpu.VMEM((own, width), F32),
+            pltpu.VMEM((own, width), F32),
+            pltpu.VMEM((1, width), F32),
+            pltpu.VMEM((width, LANES), BF16),
+            pltpu.VMEM((own, LANES), F32),
             pltpu.VMEM((tiles, n * own), BF16),
             pltpu.VMEM((2, n * own, tiles), BF16),
             pltpu.VMEM((PARTS, tiles // pack // 2, 2 * pack * chains // PARTS, 2 * LANES), BF16),
@@ -575,19 +605,16 @@
             pltpu.VMEM((chains, tiles, LANES), F32),
             pltpu.VMEM((n * own, width // PARTS), F32),
             pltpu.VMEM((n * own, width // PARTS), BF16),
-            pltpu.VMEM((n * own, width // PARTS + LANES), BF16),
+            pltpu.VMEM((n * own, width // PARTS), BF16),
+            pltpu.VMEM((n * own, LANES), BF16),
             pltpu.VMEM((n, own, width // PARTS), BF16),
-            pltpu.VMEM((n, own, width // PARTS + LANES), BF16),
+            pltpu.VMEM((n, own, width // PARTS), BF16),
+            pltpu.VMEM((n, own, LANES), BF16),
             pltpu.VMEM((own, LANES), F32),
             pltpu.VMEM((nf, own, LANES), F32),
             dma((10,)),
-            dma((1,)), dma((1,)),
-            dma((2,)), dma((PARTS,)), dma((PARTS, n)),
-            dma((1,)), dma((units,)),
-            dma((1,)), dma((units,)),
-            dma((1,)), dma((units,)),
-            dma((PARTS,)), dma((PARTS,)),
-            dma((1,)), dma((1,)),
+            dma((1,)), dma((PARTS,)), dma((PARTS, max(n, units))),
+            dma((units,)), dma((units,)), dma((PARTS + 1,)), dma((1,)),
         ],
         compiler_params=pltpu.CompilerParams(collective_id=0, has_side_effects=True),
     )(

time: 29.2 us -> 28.7 us (0.983)
  Pallas kernels: 28.4 us -> 27.9 us
    pallas_call x1, Pallas kernels: 27.7 us -> 27.3 us  [body(): pl.pallas_call(functools.partial(kernel, n, nf, chains, quarter), out_sha...]
where the time goes in v4:
time: 28.7 us; the launch traced here: 28.6 us
  Pallas kernels  27.9 us (97%)
  between operations  0.64 us (2%)
    pallas_call x1, Pallas kernels, body(): pl.pallas_call(functools.partial(kernel, n, nf, chains, quarter), out_sha...  27.3 us
    pallas_call x1, Pallas kernels, body(): pl.pallas_call(finish, out_shape=tuple((jax.ShapeDtypeStruct(x.shape, x.d...  0.68 us

profile of v4, /device:TPU:0, one launch (start us, length us, event | category | flops | bytes accessed | tf_op | source)
XLA Modules:
  0.0 28.6 jit_solution(15829566138837667589)
XLA Ops:
  0.6 27.3 %shard_map.129 = (f32[16,512]{1,0:T(8,128)S(1)}, f32[16,512]{1,0:T(8,128)S(1)}, f32[16,512]{1,0:T(8,128)S(1)}, f32[16,16]{1,0:T(8,128)S(1)}) custom-call(bf16[16,256,128]{2,1,0:T(8,128)(2,1)} %bitcast.6, s32[128,128]{1,0:T(8,128)} %lab_hbm.1, s32[1,128]{1,0:T(1,128)} %bitcast.8, s32[1,128]{1,0:T(1,128)} %bitcast.9, f32[16,512]{1,0:T(8,128)} %pos_hbm.1, ...), custom_call_target="tpu_custom_call" | custom-call | tf_op jit(solution)/shard_map/pallas_call | solution.py:568
  27.9 0.7 %shard_map.130 = (f32[16,512]{1,0:T(8,128)}, f32[16,512]{1,0:T(8,128)}, f32[16,512]{1,0:T(8,128)}, f32[16,16]{1,0:T(8,128)}) custom-call(f32[16,512]{1,0:T(8,128)S(1)} %get-tuple-element.8.refs_0_, f32[16,512]{1,0:T(8,128)S(1)} %get-tuple-element.9.refs_1_, f32[16,512]{1,0:T(8,128)S(1)} %get-tuple-element.10.refs_2_, f32[16,16]{1,0:T(8,128)S(1)} %get-tuple-element.11.refs_3_), custom_call_target="tpu_custom_call" | custom-call | tf_op jit(solution)/shard_map/pallas_call | solution.py:626

commit v5 on v4

--- a/solution.py
+++ b/solution.py
@@ -33,9 +33,9 @@
     obs_hbm, lab_hbm, live_hbm, grp_hbm, pos_hbm, mom_hbm, grad_hbm, mean_hbm, prec_hbm, mass_hbm,
     newpos_ref, newmom_ref, newgrad_ref, energy_ref,
     lab_in, live_ref, grp_ref, pos_ref, mom_ref, grad_ref, mean_ref, pair_ref,
-    lab_ref, par_ref, obs, perm, back, hand, wall, half_ref, drift_ref, lane_mass_ref, gather_ref, e0_ref, hot_ref, sum_ref, lhs, mine, pair_send, pair_recv,
+    lab_ref, par_ref, obs, perm, back, hand, wall, half_ref, state_ref, tot_send, tot_recv, gather_ref, hot_ref, sum_ref, lhs, mine, pair_send, pair_recv,
     far_send, far_recv, res_own, res_recv, nll_ref, dmat, acc, gsend0, gsend1, nsend, grecv0, grecv1, nrecv, esend, erecv,
-    in_sem, h_rsem, w_rsem, t_sem, p_rsem, f_rsem, g_rsem, e_rsem,
+    in_sem, h_rsem, w_rsem, t_sem, p_rsem, f_rsem, g_rsem, e_rsem, s_rsem,
 ):
     h_ssem, w_ssem, p_ssem, f_ssem = (in_sem.at[i:j] for i, j in ((0, 1), (1, 3), (3, 4), (4, 5)))
     r_ssem, g_ssem, e_ssem = (in_sem.at[i:j] for i, j in ((5, 6), (6, 9), (9, 10)))
@@ -82,6 +82,7 @@
         pl.semaphore_signal(barrier, inc=1, device_id={"dp": d}, device_id_type=MESH)
 
     leads = bit == 1
+    follows = bit == 0
 
     @pl.when(leads)
     def _():
@@ -210,11 +211,12 @@
     packed = jnp.dot(
         jnp.concatenate([high, rest, low], axis=0), perm[...], preferred_element_type=F32
     )
-    drift_ref[...] = packed[:own] + packed[own:2 * own] + packed[2 * own:]
-    lane_mass_ref[...] = jnp.dot(
+    state_ref[0, :own, :] = packed[:own] + packed[own:2 * own] + packed[2 * own:]
+    lane_mass = jnp.dot(
         pair_ref[...], (iota((quarter, width), 0) == iota((quarter, width), 1) % quarter).astype(F32),
         precision=lax.Precision.HIGHEST, preferred_element_type=F32,
     )[1:2, :]
+    state_ref[0, own:own + 8, :] = jnp.broadcast_to(0.5 * lane_mass, (8, width))
     gather_ref[...] = (
         iota((width, LANES), 0) // quarter == iota((width, LANES), 1)
     ).astype(F32).astype(BF16)
@@ -226,8 +228,10 @@
     while shift >= chains:
         e0 = e0 + pltpu.roll(e0, shift, 1)
         shift //= 2
-    e0_ref[...] = e0
+    state_ref[0, own + 8:, :] = jnp.concatenate([e0] * (width // LANES), axis=1)
     fetches[9].wait()
+    state_copy = remote(state_ref.at[0], state_ref.at[1], e_ssem.at[0], s_rsem.at[0], {"feat": near})
+    pl.when(follows)(lambda: state_copy.start())
 
     half_tiles = tiles // 2
     row_t, lane_t = iota((tiles, LANES), 0), iota((tiles, LANES), 1)
@@ -441,22 +445,23 @@
         over_groups(body)
 
     def g_copy(h, to):
-        return pltpu.make_async_remote_copy(
-            src_ref=sums[h][0].at[block(to)], dst_ref=sums[h][1].at[me],
-            send_sem=g_ssem.at[h], recv_sem=g_rsem.at[h],
-            device_id={"dp": to}, device_id_type=MESH,
+        return remote(
+            sums[h][0].at[block(to)], sums[h][1].at[1 - bit, me], g_ssem.at[h], g_rsem.at[1 - bit, h],
+            {"dp": to, "feat": feat + 1 - bit},
         )
 
-    def g_all(h):
-        return pltpu.make_async_remote_copy(
-            src_ref=sums[h][1].at[pl.ds(0, n - 1)], dst_ref=sums[h][1].at[pl.ds(0, n - 1)],
-            send_sem=g_ssem.at[h], recv_sem=g_rsem.at[h],
-            device_id={"dp": (me + 1) % n}, device_id_type=MESH,
-        )
+    def g_all(h, side, count):
+        got = sums[h][1].at[side, pl.ds(0, count)]
+        return remote(got, got, g_ssem.at[h], g_rsem.at[side, h], {"feat": near})
 
     def send_sums(h):
         others(lambda d: g_copy(h, d).start())
-        sums[h][1][me] = sums[h][0][block(me), :]
+
+        @pl.when(leads)
+        def _():
+            sums[h][1][0, me] = sums[h][0][block(me), :]
+
+        pl.when(follows)(lambda: g_copy(h, me).start())
 
     lag = 2
     for u in range(units):
@@ -481,9 +486,9 @@
     finish_half(PARTS - 1)
     send_sums(PARTS - 1)
 
-    def total_of(h):
-        g_all(h).wait_recv()
-        return jnp.sum(sums[h][1][...].astype(F32), axis=0)
+    def total_of(h, side):
+        g_all(h, side, n - 1 + side).wait_recv()
+        return jnp.sum(sums[h][1][side].astype(F32), axis=0)
 
     def natural(packed, h):
         parts = jnp.concatenate(split(packed), axis=0)
@@ -492,55 +497,79 @@
         )
         return both[:own] + both[own:]
 
-    energy = e0_ref[...]
-    totals = []
-    for h in range(PARTS):
-        if h == PARTS - 1:
-            loss = total_of(PARTS)
-            energy = energy + loss + pltpu.roll(loss, LANES - chains, 1)
-        totals.append(total_of(h))
-        cols = slice(h * part_width, (h + 1) * part_width)
-        t = drift_ref[:, cols] - 0.5 * step_size * totals[h]
-        parts = stacked(0.5 * lane_mass_ref[:, cols] * t * t)
-        both = jnp.dot(parts, gather_ref[cols, :], preferred_element_type=F32)
-        energy = energy + both[:own] + both[own:]
-    esend[...] = energy
+    def write(totals):
+        new_gradient = par_ref[0:1, :] * (newpos_ref[...] - mean_ref[...])
+        for h in range(PARTS):
+            new_gradient = new_gradient + natural(totals[h], h)
+        newgrad_ref[...] = new_gradient
+        newmom_ref[...] = half_ref[...] - 0.5 * step_size * new_gradient
+
+    tot_copy = remote(tot_send, tot_recv, h_ssem.at[0], s_rsem.at[0], {"feat": near})
 
     def e_copy(i):
-        return pltpu.make_async_remote_copy(
-            src_ref=esend, dst_ref=erecv.at[feat], send_sem=e_ssem.at[0],
-            recv_sem=e_rsem.at[0], device_id={"feat": (feat + i) % nf}, device_id_type=MESH,
+        return remote(
+            esend, erecv.at[feat // 2], e_ssem.at[0], e_rsem.at[0], {"feat": (feat + i) % nf}
         )
 
-    for i in range(1, nf):
-        e_copy(i).start()
-    erecv[feat] = esend[...]
-    new_gradient = par_ref[0:1, :] * (newpos_ref[...] - mean_ref[...])
-    for h in range(PARTS):
-        new_gradient = new_gradient + natural(totals[h], h)
-    newgrad_ref[...] = new_gradient
-    newmom_ref[...] = half_ref[...] - 0.5 * step_size * new_gradient
-    for drain in (pair_drain, far_drain, res_drain):
-        drain()
-    for h in range(PARTS + 1):
-        g_all(h).wait_send()
+    def e_all(count):
+        got = erecv.at[pl.ds(0, count)]
+        return remote(got, got, e_ssem.at[0], e_rsem.at[0], {"feat": near})
+
+    def drain_all(count):
+        for drain in (pair_drain, far_drain, res_drain):
+            drain()
+        for h in range(PARTS + 1):
+            g_all(h, 0, count).wait_send()
 
     @pl.when(leads)
     def _():
+        state_copy.wait_recv()
+        energy = state_ref[0, own + 8:, :LANES] + state_ref[1, own + 8:, :LANES]
+        totals = []
+        for h in range(PARTS):
+            if h == PARTS - 1:
+                loss = total_of(PARTS, 0) + total_of(PARTS, 1)
+                energy = energy + loss + pltpu.roll(loss, LANES - chains, 1)
+            cols = slice(h * part_width, (h + 1) * part_width)
+            squares = []
+            for side in range(2):
+                total = total_of(h, side)
+                if side:
+                    tot_send[h] = total
+                else:
+                    totals.append(total)
+                t = state_ref[side, :own, cols] - 0.5 * step_size * total
+                squares.append(state_ref[side, own:own + 1, cols] * t * t)
+            both = jnp.dot(
+                stacked(squares[0] + squares[1]), gather_ref[cols, :], preferred_element_type=F32
+            )
+            energy = energy + both[:own] + both[own:]
+        esend[...] = energy
+        for i in range(1, nf):
+            e_copy(i).start()
+        tot_copy.start()
+        erecv[feat // 2] = esend[...]
+        write(totals)
+        drain_all(n - 1)
         for side in range(2):
             sent(side).wait_send()
-
-    @pl.when(jnp.logical_not(leads))
+        tot_copy.wait_send()
+        sent_e = state_ref.at[1, pl.ds(0, 8 * (nf - 1)), pl.ds(0, own * LANES // 8)]
+        remote(sent_e, sent_e, e_ssem.at[0], e_rsem.at[0], {"feat": near}).wait_send()
+        if nf > 2:
+            e_all(nf // 2 - 1).wait_recv()
+
+    @pl.when(follows)
     def _():
+        tot_copy.wait_recv()
+        write([tot_recv[h] for h in range(PARTS)])
+        drain_all(n)
         hand_all.wait_send()
-
-    pltpu.make_async_remote_copy(
-        src_ref=erecv.at[pl.ds(0, nf - 1)], dst_ref=erecv.at[pl.ds(0, nf - 1)],
-        send_sem=e_ssem.at[0], recv_sem=e_rsem.at[0],
-        device_id={"feat": near}, device_id_type=MESH,
-    ).wait()
+        state_copy.wait_send()
+        e_all(nf // 2).wait_recv()
+
     e = erecv[0]
-    for i in range(1, nf):
+    for i in range(1, nf // 2):
         e = e + erecv[i]
     energy_ref[...] = e[:, :chains]
 
@@ -587,10 +616,10 @@
             pltpu.VMEM((PARTS, own, width // PARTS), BF16),
             pltpu.VMEM((2, PARTS, n * own, width // PARTS), BF16),
             pltpu.VMEM((own, width), F32),
-            pltpu.VMEM((own, width), F32),
-            pltpu.VMEM((1, width), F32),
+            pltpu.VMEM((2, 2 * own + 8, width), F32),
+            pltpu.VMEM((PARTS, own, width // PARTS), F32),
+            pltpu.VMEM((PARTS, own, width // PARTS), F32),
             pltpu.VMEM((width, LANES), BF16),
-            pltpu.VMEM((own, LANES), F32),
             pltpu.VMEM((tiles, n * own), BF16),
             pltpu.VMEM((2, n * own, tiles), BF16),
             pltpu.VMEM((PARTS, tiles // pack // 2, 2 * pack * chains // PARTS, 2 * LANES), BF16),
@@ -607,14 +636,14 @@
             pltpu.VMEM((n * own, width // PARTS), BF16),
             pltpu.VMEM((n * own, width // PARTS), BF16),
             pltpu.VMEM((n * own, LANES), BF16),
-            pltpu.VMEM((n, own, width // PARTS), BF16),
-            pltpu.VMEM((n, own, width // PARTS), BF16),
-            pltpu.VMEM((n, own, LANES), BF16),
+            pltpu.VMEM((2, n, own, width // PARTS), BF16),
+            pltpu.VMEM((2, n, own, width // PARTS), BF16),
+            pltpu.VMEM((2, n, own, LANES), BF16),
             pltpu.VMEM((own, LANES), F32),
-            pltpu.VMEM((nf, own, LANES), F32),
+            pltpu.VMEM((nf // 2, own, LANES), F32),
             dma((10,)),
             dma((1,)), dma((PARTS,)), dma((PARTS, max(n, units))),
-            dma((units,)), dma((units,)), dma((PARTS + 1,)), dma((1,)),
+            dma((units,)), dma((units,)), dma((2, PARTS + 1)), dma((1,)), dma((1,)),
         ],
         compiler_params=pltpu.CompilerParams(collective_id=0, has_side_effects=True),
     )(

time: 28.7 us -> 28 us (0.976)
  Pallas kernels: 27.9 us -> 27.2 us
    pallas_call x1, Pallas kernels: 27.3 us -> 26.5 us  [body(): pl.pallas_call(functools.partial(kernel, n, nf, chains, quarter), out_sha...]
where the time goes in v5:
time: 28 us; the launch traced here: 27.8 us
  Pallas kernels  27.2 us (97%)
  between operations  0.64 us (2%)
    pallas_call x1, Pallas kernels, body(): pl.pallas_call(functools.partial(kernel, n, nf, chains, quarter), out_sha...  26.5 us
    pallas_call x1, Pallas kernels, body(): pl.pallas_call(finish, out_shape=tuple((jax.ShapeDtypeStruct(x.shape, x.d...  0.68 us

profile of v5, /device:TPU:0, one launch (start us, length us, event | category | flops | bytes accessed | tf_op | source)
XLA Modules:
  0.0 27.8 jit_solution(3170296402375502262)
XLA Ops:
  0.6 26.5 %shard_map.129 = (f32[16,512]{1,0:T(8,128)S(1)}, f32[16,512]{1,0:T(8,128)S(1)}, f32[16,512]{1,0:T(8,128)S(1)}, f32[16,16]{1,0:T(8,128)S(1)}) custom-call(bf16[16,256,128]{2,1,0:T(8,128)(2,1)} %bitcast.6, s32[128,128]{1,0:T(8,128)} %lab_hbm.1, s32[1,128]{1,0:T(1,128)} %bitcast.8, s32[1,128]{1,0:T(1,128)} %bitcast.9, f32[16,512]{1,0:T(8,128)} %pos_hbm.1, ...), custom_call_target="tpu_custom_call" | custom-call | tf_op jit(solution)/shard_map/pallas_call | solution.py:597
  27.2 0.7 %shard_map.130 = (f32[16,512]{1,0:T(8,128)}, f32[16,512]{1,0:T(8,128)}, f32[16,512]{1,0:T(8,128)}, f32[16,16]{1,0:T(8,128)}) custom-call(f32[16,512]{1,0:T(8,128)S(1)} %get-tuple-element.8.refs_0_, f32[16,512]{1,0:T(8,128)S(1)} %get-tuple-element.9.refs_1_, f32[16,512]{1,0:T(8,128)S(1)} %get-tuple-element.10.refs_2_, f32[16,16]{1,0:T(8,128)S(1)} %get-tuple-element.11.refs_3_), custom_call_target="tpu_custom_call" | custom-call | tf_op jit(solution)/shard_map/pallas_call | solution.py:655

commit v6 on v5

--- a/solution.py
+++ b/solution.py
@@ -33,7 +33,7 @@
     obs_hbm, lab_hbm, live_hbm, grp_hbm, pos_hbm, mom_hbm, grad_hbm, mean_hbm, prec_hbm, mass_hbm,
     newpos_ref, newmom_ref, newgrad_ref, energy_ref,
     lab_in, live_ref, grp_ref, pos_ref, mom_ref, grad_ref, mean_ref, pair_ref,
-    lab_ref, par_ref, obs, perm, back, hand, wall, half_ref, state_ref, tot_send, tot_recv, gather_ref, hot_ref, sum_ref, lhs, mine, pair_send, pair_recv,
+    lab_ref, par_ref, obs, perm, back, hand, wall, half_ref, state_ref, tot_send, tot_recv, gather_ref, hot_ref, sum_ref, most_ref, last_ref, lhs, mine, pair_send, pair_recv,
     far_send, far_recv, res_own, res_recv, nll_ref, dmat, acc, gsend0, gsend1, nsend, grecv0, grecv1, nrecv, esend, erecv,
     in_sem, h_rsem, w_rsem, t_sem, p_rsem, f_rsem, g_rsem, e_rsem, s_rsem,
 ):
@@ -199,6 +199,8 @@
     for i in range(2):
         side = member[:, i * (tiles // 2):(i + 1) * (tiles // 2)]
         sum_ref[i] = jnp.concatenate([side, side], axis=1)
+        most_ref[i] = jnp.concatenate([side[:, :-chunk_tiles]] * 2, axis=1)
+        last_ref[i] = jnp.concatenate([side[:, -chunk_tiles:]] * 2, axis=1)
     lab_ref[...] = jnp.where(
         iota(lab_ref.shape, 1).astype(F32) < column(live_ref[...]), lab_in[...].astype(F32), -1.0
     )
@@ -374,7 +376,7 @@
             return xs[0]
         half = len(xs) // 2
         shift = half * width
-        low = lane_g % len(xs) < half
+        low = lane_g[:xs[0].shape[0]] % len(xs) < half
         pairs = []
         for a, b in zip(xs[:half], xs[half:]):
             other = jnp.where(low, b, a)
@@ -387,12 +389,13 @@
             pairs.append(jnp.where(low, a, b) + moved)
         return fold(pairs, width)
 
-    def compact(h, first):
+    def compact(h, first, start=0, count=None):
+        count = count or half_tiles
         out = []
         for m in range(blocks):
             xs = []
             for j in range(pack):
-                tile = pl.ds(pl.multiple_of(first, half_tiles), half_tiles)
+                tile = pl.ds(pl.multiple_of(first + start, octet), count)
                 xs.append(dmat[h * part_chains + m * pack + j, tile, :])
             out.append(fold(xs, quarter))
         return stacked(jnp.concatenate(out, axis=1))
@@ -410,19 +413,28 @@
     def member_dot(side, out, rhs):
         return jnp.dot(sum_ref[side, out, :], rhs, preferred_element_type=F32)
 
+    most = half_tiles - chunk_tiles
+
     def start_half(h):
         rhs = compact(h, mine_first)
+        rest = compact(h, near_first, 0, most)
         nll = None
         if h == PARTS - 1:
             nll = stacked(nll_ref[pl.ds(pl.multiple_of(mine_first, half_tiles), half_tiles), :])
 
         def body(out):
-            acc[out, :] = member_dot(bit, out, rhs)
+            acc[out, :] = member_dot(bit, out, rhs) + jnp.dot(
+                most_ref[1 - bit, out, :], rest, preferred_element_type=F32
+            )
             if nll is not None:
                 hi, lo = split(member_dot(bit, out, nll))
-                nsend[out, :] = (
-                    hi.astype(F32) + pltpu.roll(lo.astype(F32), chains, 1)
-                ).astype(BF16)
+                loss = hi.astype(F32) + pltpu.roll(lo.astype(F32), chains, 1)
+                loss = loss.reshape(seg_groups // own, 2, own // 2, LANES)
+                loss = loss[:, 0].reshape(-1, LANES) + pltpu.roll(
+                    loss[:, 1].reshape(-1, LANES), 2 * chains, 1
+                )
+                owners = pl.ds(out.start // own, seg_groups // own)
+                nsend[owners] = loss.reshape(-1, own // 2, LANES).astype(BF16)
 
         over_groups(body)
 
@@ -437,16 +449,17 @@
         over_groups(body)
 
     def finish_half(h):
-        rhs = compact(h, near_first)
+        rhs = compact(h, near_first, most, chunk_tiles)
 
         def body(out):
-            sums[h][0][out, :] = (acc[out, :] + member_dot(1 - bit, out, rhs)).astype(BF16)
+            sums[h][0][out, :] = (acc[out, :] + jnp.dot(last_ref[1 - bit, out, :], rhs, preferred_element_type=F32)).astype(BF16)
 
         over_groups(body)
 
     def g_copy(h, to):
+        src = nsend.at[to] if h == PARTS else sums[h][0].at[block(to)]
         return remote(
-            sums[h][0].at[block(to)], sums[h][1].at[1 - bit, me], g_ssem.at[h], g_rsem.at[1 - bit, h],
+            src, sums[h][1].at[1 - bit, me], g_ssem.at[h], g_rsem.at[1 - bit, h],
             {"dp": to, "feat": feat + 1 - bit},
         )
 
@@ -455,34 +468,39 @@
         return remote(got, got, g_ssem.at[h], g_rsem.at[side, h], {"feat": near})
 
     def send_sums(h):
-        others(lambda d: g_copy(h, d).start())
+        below(lambda d: g_copy(h, d).start())
+        above(lambda d: g_copy(h, d).start())
 
         @pl.when(leads)
         def _():
-            sums[h][1][0, me] = sums[h][0][block(me), :]
+            sums[h][1][0, me] = nsend[me] if h == PARTS else sums[h][0][block(me), :]
 
         pl.when(follows)(lambda: g_copy(h, me).start())
 
     lag = 2
+
+    def near_step(u):
+        res_copy(u).wait_recv()
+        near_grads(u)
+
     for u in range(units):
+        if u == units - 1:
+            near_step(u - lag)
         far_copy(u).wait_recv()
-        if u >= lag:
+        if lag <= u < units - 1:
             res_copy(u - lag).wait_recv()
         residual(u)
         mine_grads(u)
-        if u >= lag:
+        if lag <= u < units - 1:
             near_grads(u - lag)
             h, k = divmod(u - lag, CHUNKS)
             if k == CHUNKS - 1:
                 whole(h)
                 send_sums(h)
-    for u in range(units - lag, units - 1):
-        res_copy(u).wait_recv()
-        near_grads(u)
+    near_step(units - 2)
     start_half(PARTS - 1)
     send_sums(PARTS)
-    res_copy(units - 1).wait_recv()
-    near_grads(units - 1)
+    near_step(units - 1)
     finish_half(PARTS - 1)
     send_sums(PARTS - 1)
 
@@ -529,6 +547,7 @@
         for h in range(PARTS):
             if h == PARTS - 1:
                 loss = total_of(PARTS, 0) + total_of(PARTS, 1)
+                loss = jnp.concatenate([loss, pltpu.roll(loss, LANES - 2 * chains, 1)], axis=0)
                 energy = energy + loss + pltpu.roll(loss, LANES - chains, 1)
             cols = slice(h * part_width, (h + 1) * part_width)
             squares = []
@@ -622,6 +641,8 @@
             pltpu.VMEM((width, LANES), BF16),
             pltpu.VMEM((tiles, n * own), BF16),
             pltpu.VMEM((2, n * own, tiles), BF16),
+            pltpu.VMEM((2, n * own, tiles - tiles // CHUNKS), BF16),
+            pltpu.VMEM((2, n * own, tiles // CHUNKS), BF16),
             pltpu.VMEM((PARTS, tiles // pack // 2, 2 * pack * chains // PARTS, 2 * LANES), BF16),
             pltpu.VMEM((half_rows, row_count), F32),
             pltpu.VMEM((half_rows, row_count), F32),
@@ -635,10 +656,10 @@
             pltpu.VMEM((n * own, width // PARTS), F32),
             pltpu.VMEM((n * own, width // PARTS), BF16),
             pltpu.VMEM((n * own, width // PARTS), BF16),
-            pltpu.VMEM((n * own, LANES), BF16),
+            pltpu.VMEM((n, own // 2, LANES), BF16),
             pltpu.VMEM((2, n, own, width // PARTS), BF16),
             pltpu.VMEM((2, n, own, width // PARTS), BF16),
-            pltpu.VMEM((2, n, own, LANES), BF16),
+            pltpu.VMEM((2, n, own // 2, LANES), BF16),
             pltpu.VMEM((own, LANES), F32),
             pltpu.VMEM((nf // 2, own, LANES), F32),
             dma((10,)),

time: 28 us -> 27.9 us (level)
  no operation moved by 1% of the time
where the time goes in v6:
time: 27.9 us; the launch traced here: 27.7 us
  Pallas kernels  27.1 us (97%)
  between operations  0.64 us (2%)
    pallas_call x1, Pallas kernels, body(): pl.pallas_call(functools.partial(kernel, n, nf, chains, quarter), out_sha...  26.4 us
    pallas_call x1, Pallas kernels, body(): pl.pallas_call(finish, out_shape=tuple((jax.ShapeDtypeStruct(x.shape, x.d...  0.68 us

profile of v6, /device:TPU:0, one launch (start us, length us, event | category | flops | bytes accessed | tf_op | source)
XLA Modules:
  0.0 27.7 jit_solution(5349581111610970536)
XLA Ops:
  0.6 26.4 %shard_map.129 = (f32[16,512]{1,0:T(8,128)S(1)}, f32[16,512]{1,0:T(8,128)S(1)}, f32[16,512]{1,0:T(8,128)S(1)}, f32[16,16]{1,0:T(8,128)S(1)}) custom-call(bf16[16,256,128]{2,1,0:T(8,128)(2,1)} %bitcast.6, s32[128,128]{1,0:T(8,128)} %lab_hbm.1, s32[1,128]{1,0:T(1,128)} %bitcast.8, s32[1,128]{1,0:T(1,128)} %bitcast.9, f32[16,512]{1,0:T(8,128)} %pos_hbm.1, ...), custom_call_target="tpu_custom_call" | custom-call | tf_op jit(solution)/shard_map/pallas_call | solution.py:616
  27.0 0.7 %shard_map.130 = (f32[16,512]{1,0:T(8,128)}, f32[16,512]{1,0:T(8,128)}, f32[16,512]{1,0:T(8,128)}, f32[16,16]{1,0:T(8,128)}) custom-call(f32[16,512]{1,0:T(8,128)S(1)} %get-tuple-element.8.refs_0_, f32[16,512]{1,0:T(8,128)S(1)} %get-tuple-element.9.refs_1_, f32[16,512]{1,0:T(8,128)S(1)} %get-tuple-element.10.refs_2_, f32[16,16]{1,0:T(8,128)S(1)} %get-tuple-element.11.refs_3_), custom_call_target="tpu_custom_call" | custom-call | tf_op jit(solution)/shard_map/pallas_call | solution.py:676

commit v7 on v6

--- a/solution.py
+++ b/solution.py
@@ -418,24 +418,10 @@
     def start_half(h):
         rhs = compact(h, mine_first)
         rest = compact(h, near_first, 0, most)
-        nll = None
-        if h == PARTS - 1:
-            nll = stacked(nll_ref[pl.ds(pl.multiple_of(mine_first, half_tiles), half_tiles), :])
-
         def body(out):
             acc[out, :] = member_dot(bit, out, rhs) + jnp.dot(
                 most_ref[1 - bit, out, :], rest, preferred_element_type=F32
             )
-            if nll is not None:
-                hi, lo = split(member_dot(bit, out, nll))
-                loss = hi.astype(F32) + pltpu.roll(lo.astype(F32), chains, 1)
-                loss = loss.reshape(seg_groups // own, 2, own // 2, LANES)
-                loss = loss[:, 0].reshape(-1, LANES) + pltpu.roll(
-                    loss[:, 1].reshape(-1, LANES), 2 * chains, 1
-                )
-                owners = pl.ds(out.start // own, seg_groups // own)
-                nsend[owners] = loss.reshape(-1, own // 2, LANES).astype(BF16)
-
         over_groups(body)
 
     def whole(h):
@@ -476,6 +462,22 @@
             sums[h][1][0, me] = nsend[me] if h == PARTS else sums[h][0][block(me), :]
 
         pl.when(follows)(lambda: g_copy(h, me).start())
+
+    def loss_sums():
+        nll = stacked(nll_ref[pl.ds(pl.multiple_of(mine_first, half_tiles), half_tiles), :])
+
+        def body(out):
+            hi, lo = split(member_dot(bit, out, nll))
+            loss = hi.astype(F32) + pltpu.roll(lo.astype(F32), chains, 1)
+            loss = loss.reshape(seg_groups // own, 2, own // 2, LANES)
+            loss = loss[:, 0].reshape(-1, LANES) + pltpu.roll(
+                loss[:, 1].reshape(-1, LANES), 2 * chains, 1
+            )
+            owners = pl.ds(out.start // own, seg_groups // own)
+            nsend[owners] = loss.reshape(-1, own // 2, LANES).astype(BF16)
+
+        over_groups(body)
+        send_sums(PARTS)
 
     lag = 2
 
@@ -490,6 +492,8 @@
         if lag <= u < units - 1:
             res_copy(u - lag).wait_recv()
         residual(u)
+        if u == units - 1:
+            loss_sums()
         mine_grads(u)
         if lag <= u < units - 1:
             near_grads(u - lag)
@@ -499,7 +503,6 @@
                 send_sums(h)
     near_step(units - 2)
     start_half(PARTS - 1)
-    send_sums(PARTS)
     near_step(units - 1)
     finish_half(PARTS - 1)
     send_sums(PARTS - 1)

time: 27.9 us -> 27.9 us (level)
  no operation moved by 1% of the time
where the time goes in v7:
time: 27.9 us; the launch traced here: 27.7 us
  Pallas kernels  27.1 us (97%)
  between operations  0.64 us (2%)
    pallas_call x1, Pallas kernels, body(): pl.pallas_call(functools.partial(kernel, n, nf, chains, quarter), out_sha...  26.4 us
    pallas_call x1, Pallas kernels, body(): pl.pallas_call(finish, out_shape=tuple((jax.ShapeDtypeStruct(x.shape, x.d...  0.68 us

profile of v7, /device:TPU:0, one launch (start us, length us, event | category | flops | bytes accessed | tf_op | source)
XLA Modules:
  0.0 27.7 jit_solution(4985324538018941658)
XLA Ops:
  0.6 26.4 %shard_map.129 = (f32[16,512]{1,0:T(8,128)S(1)}, f32[16,512]{1,0:T(8,128)S(1)}, f32[16,512]{1,0:T(8,128)S(1)}, f32[16,16]{1,0:T(8,128)S(1)}) custom-call(bf16[16,256,128]{2,1,0:T(8,128)(2,1)} %bitcast.6, s32[128,128]{1,0:T(8,128)} %lab_hbm.1, s32[1,128]{1,0:T(1,128)} %bitcast.8, s32[1,128]{1,0:T(1,128)} %bitcast.9, f32[16,512]{1,0:T(8,128)} %pos_hbm.1, ...), custom_call_target="tpu_custom_call" | custom-call | tf_op jit(solution)/shard_map/pallas_call | solution.py:619
  27.1 0.7 %shard_map.130 = (f32[16,512]{1,0:T(8,128)}, f32[16,512]{1,0:T(8,128)}, f32[16,512]{1,0:T(8,128)}, f32[16,16]{1,0:T(8,128)}) custom-call(f32[16,512]{1,0:T(8,128)S(1)} %get-tuple-element.8.refs_0_, f32[16,512]{1,0:T(8,128)S(1)} %get-tuple-element.9.refs_1_, f32[16,512]{1,0:T(8,128)S(1)} %get-tuple-element.10.refs_2_, f32[16,16]{1,0:T(8,128)S(1)} %get-tuple-element.11.refs_3_), custom_call_target="tpu_custom_call" | custom-call | tf_op jit(solution)/shard_map/pallas_call | solution.py:679
